TPU v7x, 8 devices: a whole 2x2x1 slice. The times are simulated.
8 devices in a mesh: frag: 1 (over z), dev: 8 (over y, x, core).
Axes of the slice: x: 2, y: 2, z: 1, core: 2. Of those that a mesh axis runs over, the one named last changes fastest.
Arguments:
- ao_ints: bfloat16 [120, 120, 120, 120], P(('frag', 'dev'))
- c_occ: bfloat16 [120, 8], P('frag')
- c_vir: bfloat16 [120, 108], P('frag')
Outputs:
- output 1: float32 [108, 108, 64], P('frag', None, 'dev')
- output 2: float32 [8, 108, 864], P('frag', None, 'dev')
All inputs are finite; a program needn't handle non-finite values.
Results may differ from a plain program's by a relative error of at most 0.001.
Values are sent between devices in bfloat16 or wider.
A program may use at most 1 GiB of HBM per device.

v0:
```python
import jax
import jax.numpy as jnp
from jax import lax
from jax.sharding import PartitionSpec as P


def solution(mesh):
    def local_part(ao_rows, c_occ, c_vir):
        n_rows = ao_rows.shape[0]
        n_ao = ao_rows.shape[1]
        n_occ = c_occ.shape[1]
        n_vir = c_vir.shape[1]
        quarter = jnp.einsum('pqrs,rx->pqsx', ao_rows, c_occ, preferred_element_type=jnp.float32).astype(jnp.bfloat16)
        half_oo = jnp.einsum('pqsx,sj->pqxj', quarter, c_occ, preferred_element_type=jnp.float32).astype(jnp.bfloat16)
        half_ov = jnp.einsum('pqsx,sb->pqxb', quarter, c_vir, preferred_element_type=jnp.float32).astype(jnp.bfloat16)
        half_oo = half_oo.reshape(n_rows, n_ao, n_occ * n_occ)
        half_ov = half_ov.reshape(n_rows, n_ao, n_occ * n_vir)
        full_oo = lax.all_to_all(half_oo, 'dev', 2, 0, tiled=True)
        full_ov = lax.all_to_all(half_ov, 'dev', 2, 0, tiled=True)
        mid_oo = jnp.einsum('qrn,rc->qcn', full_oo, c_vir, preferred_element_type=jnp.float32).astype(jnp.bfloat16)
        mid_ov = jnp.einsum('qrn,rb->qbn', full_ov, c_vir, preferred_element_type=jnp.float32).astype(jnp.bfloat16)
        v_abij = jnp.einsum('pa,pbm->abm', c_vir, mid_oo, preferred_element_type=jnp.float32)
        v_iajb = jnp.einsum('pi,pam->iam', c_occ, mid_ov, preferred_element_type=jnp.float32)
        return v_abij, v_iajb

    return jax.shard_map(local_part, mesh=mesh,
                         in_specs=(P(('frag', 'dev')), P('frag'), P('frag')),
                         out_specs=(P('frag', None, 'dev'), P('frag', None, 'dev')),
                         check_vma=False)
```

profile of v0, /device:TPU:0, one launch (start us, length us, event | category | flops | bytes accessed | tf_op | source)
XLA Modules:
  0.0 99.2 jit_solution(12866124185611074575)
XLA Ops:
  0.6 0.0 copy-start
  0.6 0.0 copy-start.2
  0.7 22.4 %convolution_convert_fusion = bf16[15,120,120,8]{2,3,1,0:T(8,128)(2,1)S(1)} fusion(bf16[15,120,120,120]{3,2,1,0:T(8,128)(2,1)} %param.3, bf16[120,8]{0,1:T(8,128)(2,1)} %param.4), kind=kOutput, calls=%fused_computation.5 | convolution fusion | flops 416448000 | bytes 55297920 | tf_op jit(solution)/shard_map/pqrs,rx->pqsx/dot_general | solution.py:13
  23.1 0.0 copy-start.1
  23.1 1.8 %copy-done.1 = bf16[15,120,120,8]{2,3,1,0:T(8,128)(2,1)} copy-done((bf16[15,120,120,8]{2,3,1,0:T(8,128)(2,1)}, bf16[15,120,120,8]{2,3,1,0:T(8,128)(2,1)S(1)}, u32[]{:S(2)}) %copy-start.1) | copy-done | bytes 3456024
  24.9 0.0 copy-done.2
  24.9 2.1 %fusion.10 = bf16[15,120,64]{1,2,0:T(8,128)(2,1)S(1)} fusion(bf16[15,120,120,8]{2,3,1,0:T(8,128)(2,1)S(1)} %convolution_convert_fusion, bf16[120,8]{0,1:T(8,128)(2,1)S(1)} %copy-done.2), kind=kOutput, calls=%fused_computation.11 | convolution fusion | flops 27763200 | bytes 3688320 | tf_op jit(solution)/shard_map/pqsx,sj->pqxj/dot_general | solution.py:14
  26.9 0.9 copy.20
  27.8 4.3 %all-to-all-start = ((bf16[15,120,64]{1,0,2:T(8,128)(2,1)}), bf16[15,120,64]{1,0,2:T(8,128)(2,1)S(1)}, u32[]{:S(2)}, u32[]{:S(2)}) async-start(bf16[15,120,64]{1,0,2:T(8,128)(2,1)} %copy.20), calls=%async_computation | async-start | bytes 524288 | tf_op jit(solution)/shard_map/all_to_all | solution.py:18
  32.1 0.0 copy-done
  32.1 4.7 %fusion.4 = bf16[15,120,8,108]{1,3,2,0:T(8,128)(2,1)S(1)} fusion(bf16[15,120,120,8]{2,3,1,0:T(8,128)(2,1)} %copy-done.1, bf16[120,108]{0,1:T(8,128)(2,1)S(1)} %copy-done), kind=kOutput, calls=%fused_computation.6 | convolution fusion | flops 374803200 | bytes 6592320 | tf_op jit(solution)/shard_map/pqsx,sb->pqxb/dot_general | solution.py:15
  36.9 4.0 %copy.33 = bf16[15,120,8,108]{1,0,3,2:T(8,128)(2,1)} copy(bf16[15,120,8,108]{1,3,2,0:T(8,128)(2,1)S(1)} %fusion.4) | data formatting | bytes 6220800 | tf_op jit(solution)/shard_map/reshape | solution.py:17
  40.9 0.0 all-to-all-done
  40.9 3.2 %all-to-all-start.1 = ((bf16[15,120,864]{1,0,2:T(8,128)(2,1)}), bf16[15,120,864]{1,0,2:T(8,128)(2,1)}, u32[]{:S(2)}, u32[]{:S(2)}) async-start(bf16[15,120,864]{1,0,2:T(8,128)(2,1)} %bitcast.46), calls=%async_computation.1 | async-start | bytes 7077888 | tf_op jit(solution)/shard_map/all_to_all | solution.py:19
  44.1 0.1 copy.22
  44.1 0.5 convolution_bitcast_fusion
  44.6 1.0 copy.29
  45.6 40.5 %all-to-all-done.1 = bf16[15,120,864]{1,0,2:T(8,128)(2,1)} async-done(((bf16[15,120,864]{1,0,2:T(8,128)(2,1)}), bf16[15,120,864]{1,0,2:T(8,128)(2,1)}, u32[]{:S(2)}, u32[]{:S(2)}) %all-to-all-start.1) | async-done | bytes 3110432 | tf_op jit(solution)/shard_map/all_to_all | solution.py:19
  86.0 2.9 %copy.27 = bf16[8,15,120,108]{2,3,1,0:T(8,128)(2,1)S(1)} copy(bf16[8,15,120,108]{2,1,3,0:T(8,128)(2,1)} %bitcast.15) | data formatting | bytes 6220800 | tf_op jit(solution)/shard_map/all_to_all | solution.py:19
  88.9 1.1 %convert_bitcast_fusion = bf16[120,108,108]{1,2,0:T(8,128)(2,1)S(1)} fusion(bf16[120,120,108]{1,2,0:T(8,128)(2,1)S(1)} %bitcast.47, bf16[120,108]{0,1:T(8,128)(2,1)S(1)} %copy-done), kind=kOutput, calls=%fused_computation | convolution fusion | flops 337322880 | bytes 5935680 | tf_op jit(solution)/shard_map/qrn,rb->qbn/dot_general | solution.py:21
  90.0 4.7 %copy.28 = bf16[120,108,108]{0,2,1:T(8,128)(2,1)} copy(bf16[120,108,108]{1,2,0:T(8,128)(2,1)S(1)} %convert_bitcast_fusion) | data formatting | bytes 5598720 | tf_op jit(solution)/shard_map/convert_element_type | solution.py:21
  94.7 4.5 %convolution_bitcast_fusion.1 = f32[8,108,108]{2,0,1:T(8,128)} fusion(bf16[120,108,108]{0,2,1:T(8,128)(2,1)} %copy.28, bf16[120,8]{0,1:T(8,128)(2,1)S(1)} %copy-done.2), kind=kOutput, calls=%fused_computation.8 | convolution fusion | flops 22394880 | bytes 3174528 | tf_op jit(solution)/shard_map/pi,pam->iam/dot_general | solution.py:23
Async XLA Ops:
  0.6 31.5 %copy-start = (bf16[120,108]{0,1:T(8,128)(2,1)S(1)}, bf16[120,108]{0,1:T(8,128)(2,1)}, u32[]{:S(2)}) copy-start(bf16[120,108]{0,1:T(8,128)(2,1)} %param.5) | copy-start | bytes 77764
  0.6 24.2 %copy-start.2 = (bf16[120,8]{0,1:T(8,128)(2,1)S(1)}, bf16[120,8]{0,1:T(8,128)(2,1)}, u32[]{:S(2)}) copy-start(bf16[120,8]{0,1:T(8,128)(2,1)} %param.4) | copy-start | bytes 5764
  23.1 1.8 %copy-start.1 = (bf16[15,120,120,8]{2,3,1,0:T(8,128)(2,1)}, bf16[15,120,120,8]{2,3,1,0:T(8,128)(2,1)S(1)}, u32[]{:S(2)}) copy-start(bf16[15,120,120,8]{2,3,1,0:T(8,128)(2,1)S(1)} %convolution_convert_fusion) | copy-start | bytes 10368004
  27.8 13.0 %all-to-all-start = ((bf16[15,120,64]{1,0,2:T(8,128)(2,1)}), bf16[15,120,64]{1,0,2:T(8,128)(2,1)S(1)}, u32[]{:S(2)}, u32[]{:S(2)}) async-start(bf16[15,120,64]{1,0,2:T(8,128)(2,1)} %copy.20), calls=%async_computation | async-start | bytes 524288 | tf_op jit(solution)/shard_map/all_to_all | solution.py:18
  40.9 45.2 %all-to-all-start.1 = ((bf16[15,120,864]{1,0,2:T(8,128)(2,1)}), bf16[15,120,864]{1,0,2:T(8,128)(2,1)}, u32[]{:S(2)}, u32[]{:S(2)}) async-start(bf16[15,120,864]{1,0,2:T(8,128)(2,1)} %bitcast.46), calls=%async_computation.1 | async-start | bytes 7077888 | tf_op jit(solution)/shard_map/all_to_all | solution.py:19
where the time goes:
time: 99.6 us; the launch traced here: 99.2 us
  waiting for transfers between devices  40.5 us (41%)
  matrix products  35.2 us (35%)
  local copies, waits for them, and re-layouts  15.3 us (15%)
  starting transfers between devices  7.51 us (8%)
    all_to_all x1, waiting for transfers between devices, local_part(): full_ov = lax.all_to_all(half_ov, 'dev', 2, 0, tiled=True)  40.5 us
    dot_general x1, matrix products, local_part(): jnp.einsum('pqrs,rx->pqsx', ao_rows, c_occ, preferred_element_type=jnp.fl...  22.4 us
    dot_general x1, matrix products, local_part(): jnp.einsum('pqsx,sb->pqxb', quarter, c_vir, preferred_element_type=jnp.fl...  4.74 us
    convert_element_type x1, local copies, waits for them, and re-layouts, local_part(): jnp.einsum('qrn,rb->qbn', full_ov, c_vir, preferred_element_type=jnp.floa...  4.72 us
    dot_general x1, matrix products, local_part(): jnp.einsum('pi,pam->iam', c_occ, mid_ov, preferred_element_type=jnp.float32)  4.46 us
    all_to_all x1, starting transfers between devices, local_part(): full_oo = lax.all_to_all(half_oo, 'dev', 2, 0, tiled=True)  4.3 us
    reshape x1, local copies, waits for them, and re-layouts, local_part(): half_ov = half_ov.reshape(n_rows, n_ao, n_occ * n_vir)  3.96 us
    all_to_all x1, starting transfers between devices, local_part(): full_ov = lax.all_to_all(half_ov, 'dev', 2, 0, tiled=True)  3.21 us
  transfers between devices with their start and end apart: 2, of which 1 were waited for; matrix products, arithmetic and copies ran while one was open for 10% of the time, Pallas kernels for 0%

commit v1 on v0

v1 whole, which is shorter than its diff:
```python
import jax
import jax.numpy as jnp
from jax import lax
from jax.experimental import pallas as pl
from jax.experimental.pallas import tpu as pltpu
from jax.sharding import PartitionSpec as P

MESH = pl.DeviceIdType.MESH
BF = jnp.bfloat16
F32 = jnp.float32
ND = 8
NP = 15
NQ = 120
NO = 8
NV = 108
ROWS = NQ * NQ
NBUF = 4
SPLIT = 5
AB = 7


def mm(a, b):
    return jnp.dot(a, b, preferred_element_type=F32)


def mm_nt(a, b):
    return lax.dot_general(a, b, (((1,), (1,)), ((), ())), preferred_element_type=F32)


def iota(shape, dim):
    return lax.broadcasted_iota(jnp.int32, shape, dim)


def one_hot(mask):
    return jnp.where(mask, 1.0, 0.0).astype(BF)


def kernel(a_ref, co_ref, cv_ref, o1_ref, o2_ref,
           abuf, tbuf, sg, rg, s1, r1, k1, k4, v1k, e6, cot, cvt, cv,
           asem, sgsem, rgsem, s1sem, r1sem):
    me = lax.axis_index('dev')
    frag = lax.axis_index('frag')

    def a_copies(p):
        slot = lax.rem(p, NBUF)
        step = ROWS // SPLIT
        return [pltpu.make_async_copy(a_ref.at[p, pl.ds(k * step, step)],
                                      abuf.at[slot, pl.ds(k * step, step)],
                                      asem.at[slot]) for k in range(SPLIT)]

    def a_start(p):
        for c in a_copies(p):
            c.start()

    def a_wait(p):
        slot = lax.rem(p, NBUF)
        pltpu.make_async_copy(a_ref.at[p], abuf.at[slot], asem.at[slot]).wait()

    for p in range(NBUF - 1):
        a_start(p)

    barrier = pltpu.get_barrier_semaphore()
    for k in range(1, ND):
        pl.semaphore_signal(barrier, inc=1, device_id=(frag, lax.rem(me + k, ND)), device_id_type=MESH)

    cot[...] = jnp.zeros(cot.shape, BF)
    cvt[...] = jnp.zeros(cvt.shape, BF)
    cot[0:NO, 0:NQ] = co_ref[...]
    cvt[0:NV, 0:NQ] = cv_ref[...]
    cv[...] = mm_nt(one_hot(iota((128, 128), 0) == iota((128, 128), 1)), cvt[...]).astype(BF)
    xr = mm(one_hot((iota((64, 16), 0) >> 3) == iota((64, 16), 1)), cot[...]).astype(BF)
    diff = iota((128, 960), 1) - iota((128, 960), 0)
    hit = diff == 0
    for k in range(1, 8):
        hit = hit | (diff == 120 * k)
    off = iota((64, 960), 1) - 120 * (iota((64, 960), 0) & 7)
    k1[...] = jnp.where((off >= 0) & (off < 120), mm(xr, one_hot(hit)), 0.0).astype(BF)
    pi = mm(one_hot((iota((128, 16), 0) & 7) == iota((128, 16), 1)), cot[...]).astype(BF)
    for c in range(15):
        col = iota((128, 128), 1)
        w = mm(pi, one_hot(iota((128, 128), 0) == (col >> 4) + 8 * c))
        k4[:, c * 128:(c + 1) * 128] = jnp.where((iota((128, 128), 0) >> 3) == (col & 15), w, 0.0).astype(BF)
    e6[...] = one_hot((iota((128, 960), 1) >> 3) == iota((128, 960), 0))

    def v1_rows(t, carry):
        row = iota((96, 128), 0) + 96 * t
        z = mm(one_hot((row >> 3) == iota((96, 128), 1)), cvt[...]).astype(BF)
        w = mm(z, e6[...])
        keep = (iota((96, 960), 0) & 7) == (iota((96, 960), 1) & 7)
        v1k[pl.ds(pl.multiple_of(96 * t, 96), 96), :] = jnp.where(keep, w, 0.0).astype(BF)
        return carry

    lax.fori_loop(0, 9, v1_rows, 0)

    pl.semaphore_wait(barrier, ND - 1)

    def step1(p):
        slot = lax.rem(p, NBUF)
        tslot = lax.rem(p, 2)
        pad = jnp.zeros((960, 8), BF)
        for g in range(8):
            left = jnp.concatenate([abuf[slot, 1920 * g:1920 * g + 960, :], pad], axis=1)
            if g < 7:
                right = jnp.concatenate([abuf[slot, 1920 * g + 960:1920 * g + 1920, :], pad], axis=1)
                out = mm(k1[...], jnp.concatenate([left, right], axis=1))
                lo = out[:, :128].reshape(8, 8, 128)
                hi = out[:, 128:].reshape(8, 8, 128)
            else:
                lo = mm(k1[...], left).reshape(8, 8, 128)
                hi = jnp.zeros((8, 8, 128), F32)
            tbuf[tslot, :, 16 * g:16 * g + 16, :] = jnp.concatenate([lo, hi], axis=1).astype(BF)

    def step23(p):
        t = tbuf[lax.rem(p, 2)].reshape(1024, 128)
        h = mm(t, cv[...]).astype(BF).reshape(8, 128, 128)
        for x in range(0, 8, 2):
            g = mm(cvt[0:112, :], jnp.concatenate([h[x], h[x + 1]], axis=1)).astype(BF)
            sg[x, p] = g[:, :128]
            sg[x + 1, p] = g[:, 128:]
        hoo = mm_nt(cot[...], t)
        hoo = jnp.concatenate([hoo[0:8, 128 * x:128 * x + 128] for x in range(8)], axis=0).astype(BF)
        s1[:, p] = mm(hoo, cv[...]).astype(BF).reshape(8, 8, 128)

    def sends(p):
        out = []
        for k in range(1, ND):
            dst = lax.rem(me + k, ND)
            out.append(pltpu.make_async_remote_copy(
                src_ref=sg.at[dst, p], dst_ref=rg.at[me, p], send_sem=sgsem.at[k], recv_sem=rgsem.at[me],
                device_id=(frag, dst), device_id_type=MESH))
            out.append(pltpu.make_async_remote_copy(
                src_ref=s1.at[dst, p], dst_ref=r1.at[me, p], send_sem=s1sem.at[k], recv_sem=r1sem.at[me],
                device_id=(frag, dst), device_id_type=MESH))
        return out

    def send(p):
        for c in sends(p):
            c.start()
        rg[me, p] = sg[me, p]
        r1[me, p] = s1[me, p]

    a_wait(0)
    a_start(NBUF - 1)
    step1(0)

    def body(p, carry):
        @pl.when(p + NBUF - 1 < NP)
        def _():
            a_start(p + NBUF - 1)

        @pl.when(p >= 2)
        def _():
            send(p - 2)

        a_wait(p)
        step1(p)
        step23(p - 1)
        return carry

    lax.fori_loop(1, NP, body, 0)
    send(NP - 2)
    step23(NP - 1)
    send(NP - 1)

    for k in range(1, ND):
        src = lax.rem(me + k, ND)
        pltpu.make_async_copy(r1.at[src], r1.at[src], r1sem.at[src]).wait()
        pltpu.make_async_copy(rg.at[src], rg.at[src], rgsem.at[src]).wait()

    v = r1[...].reshape(960, 128)

    def v1_out(t, carry):
        w = mm(v1k[pl.ds(pl.multiple_of(96 * t, 96), 96), :], v)
        o1_ref[pl.ds(12 * t, 12)] = w.reshape(12, 8, 128)[:, :, :NV]
        return carry

    lax.fori_loop(0, 9, v1_out, 0)

    for ab in range(0, AB, 2):
        left = rg[:, :, 16 * ab:16 * ab + 16, :].reshape(1920, 128)
        if ab + 1 < AB:
            right = rg[:, :, 16 * ab + 16:16 * ab + 32, :].reshape(1920, 128)
            w = mm(k4[...], jnp.concatenate([left, right], axis=1)).reshape(16, 8, 256)
            o2_ref[16 * ab:16 * ab + 16] = w[:, :, :NV]
            o2_ref[16 * ab + 16:16 * ab + 32] = w[:, :, 128:128 + NV]
        else:
            w = mm(k4[...], left).reshape(16, 8, 128)
            o2_ref[16 * ab:NV] = w[:NV - 16 * ab, :, :NV]

    for k in range(1, ND):
        dst = lax.rem(me + k, ND)
        pltpu.make_async_copy(sg.at[dst], sg.at[dst], sgsem.at[k]).wait()
        pltpu.make_async_copy(s1.at[dst], s1.at[dst], s1sem.at[k]).wait()


def solution(mesh):
    def local_part(ao, co, cv):
        a = ao.reshape(NP, ROWS, NQ)
        vm = pl.BlockSpec(memory_space=pltpu.VMEM)
        o1, o2 = pl.pallas_call(
            kernel,
            out_shape=[jax.ShapeDtypeStruct((NV, NO, NV), F32), jax.ShapeDtypeStruct((NV, NO, NV), F32)],
            in_specs=[pl.BlockSpec(memory_space=pl.ANY), vm, vm],
            out_specs=[vm, vm],
            scratch_shapes=[
                pltpu.VMEM((NBUF, ROWS, NQ), BF),
                pltpu.VMEM((2, 8, 128, 128), BF),
                pltpu.VMEM((8, NP, 112, 128), BF),
                pltpu.VMEM((8, NP, 112, 128), BF),
                pltpu.VMEM((8, NP, 8, 128), BF),
                pltpu.VMEM((8, NP, 8, 128), BF),
                pltpu.VMEM((64, 960), BF),
                pltpu.VMEM((128, 1920), BF),
                pltpu.VMEM((864, 960), BF),
                pltpu.VMEM((128, 960), BF),
                pltpu.VMEM((16, 128), BF),
                pltpu.VMEM((128, 128), BF),
                pltpu.VMEM((128, 128), BF),
                pltpu.SemaphoreType.DMA((NBUF,)),
                pltpu.SemaphoreType.DMA((ND,)),
                pltpu.SemaphoreType.DMA((ND,)),
                pltpu.SemaphoreType.DMA((ND,)),
                pltpu.SemaphoreType.DMA((ND,)),
            ],
            compiler_params=pltpu.CompilerParams(collective_id=0, has_side_effects=True,
                                                 vmem_limit_bytes=60 * 1024 * 1024),
            name='mo_blocks',
        )(a, co.T, cv.T)
        return o1.transpose(0, 2, 1), o2.transpose(1, 0, 2)

    return jax.shard_map(local_part, mesh=mesh,
                         in_specs=(P(('frag', 'dev')), P('frag'), P('frag')),
                         out_specs=(P('frag', None, 'dev'), P('frag', None, 'dev')),
                         check_vma=False)
```

time: 99.6 us -> 57.9 us (0.58)
  Pallas kernels: 0 us -> 53.5 us
  waiting for transfers between devices: 40.5 us -> 0 us
  matrix products: 35.2 us -> 0 us
  local copies, waits for them, and re-layouts: 15.3 us -> 3.61 us
  starting transfers between devices: 7.51 us -> 0 us
    pallas_call x0 -> x1, Pallas kernels: none -> 53.5 us  [local_part(): pl.pallas_call(kernel, out_shape=[jax.ShapeDtypeStruct((NV, NO, NV), F32)...]
    all_to_all x2 -> x0, waiting for transfers between devices: 40.5 us -> none  [the longest x1 40.5 us: local_part(): full_ov = lax.all_to_all(half_ov, 'dev', 2, 0, tiled=True)]
    dot_general x6 -> x0, matrix products: 35.2 us -> none  [the longest x1 22.4 us: local_part(): jnp.einsum('pqrs,rx->pqsx', ao_rows, c_occ, preferred_element_type=jnp.fl...]
    all_to_all x2 -> x0, starting transfers between devices: 7.51 us -> none  [the longest x1 4.3 us: local_part(): full_oo = lax.all_to_all(half_oo, 'dev', 2, 0, tiled=True)]
    reshape x2 -> x0, local copies, waits for them, and re-layouts: 4.86 us -> none  [the longest x1 3.96 us: local_part(): half_ov = half_ov.reshape(n_rows, n_ao, n_occ * n_vir)]
    convert_element_type x1 -> x0, local copies, waits for them, and re-layouts: 4.72 us -> none  [local_part(): jnp.einsum('qrn,rb->qbn', full_ov, c_vir, preferred_element_type=jnp.floa...]
    all_to_all x2 -> x0, local copies, waits for them, and re-layouts: 2.97 us -> none  [the longest x1 2.9 us: local_part(): full_ov = lax.all_to_all(half_ov, 'dev', 2, 0, tiled=True)]
    unnamed x7 -> x2, local copies, waits for them, and re-layouts: 2.8 us -> 3.61 us
  transfers between devices with their start and end apart: 2 -> 0, of which waited for: 1 -> 0; matrix products, arithmetic and copies ran while one was open for 10% -> 0% of each run, Pallas kernels for 0% -> 0%
where the time goes in v1:
time: 57.9 us; the launch traced here: 57.7 us
  Pallas kernels  53.5 us (92%)
  local copies, waits for them, and re-layouts  3.61 us (6%)
  between operations  0.64 us (1%)
    pallas_call x1, Pallas kernels, local_part(): pl.pallas_call(kernel, out_shape=[jax.ShapeDtypeStruct((NV, NO, NV), F32)...  53.5 us
    unnamed x2, local copies, waits for them, and re-layouts  3.61 us

profile of v1, /device:TPU:0, one launch (start us, length us, event | category | flops | bytes accessed | tf_op | source)
XLA Modules:
  0.0 57.7 jit_solution(14358448919001840108)
XLA Ops:
  0.6 53.5 %mo_blocks.1 = (f32[108,8,108]{2,1,0:T(8,128)}, f32[108,8,108]{2,1,0:T(8,128)}) custom-call(bf16[15,14400,120]{2,1,0:T(8,128)(2,1)} %bitcast.5, bf16[8,120]{1,0:T(8,128)(2,1)} %bitcast.9, bf16[108,120]{1,0:T(8,128)(2,1)} %bitcast.8), custom_call_target="tpu_custom_call" | custom-call | tf_op jit(solution)/shard_map/mo_blocks/pallas_call | solution.py:200
  54.1 1.8 %copy.7 = f32[108,108,8]{1,2,0:T(8,128)} copy(f32[108,108,8]{1,2,0:T(8,128)} %bitcast.7) | data formatting | bytes 746496
  55.9 1.8 %copy.8 = f32[8,108,108]{2,0,1:T(8,128)} copy(f32[8,108,108]{2,0,1:T(8,128)} %bitcast.6) | data formatting | bytes 746496

commit v2 on v1

--- a/solution.py
+++ b/solution.py
@@ -17,6 +17,11 @@
 NBUF = 4
 SPLIT = 5
 AB = 7
+NE = 2
+EX = 16 * NE
+RSR = 8 * (NV - EX)
+NCH = 2
+CH = RSR // (2 * NCH)
 
 
 def mm(a, b):
@@ -36,10 +41,18 @@
 
 
 def kernel(a_ref, co_ref, cv_ref, o1_ref, o2_ref,
-           abuf, tbuf, sg, rg, s1, r1, k1, k4, v1k, e6, cot, cvt, cv,
-           asem, sgsem, rgsem, s1sem, r1sem):
+           abuf, tbuf, sg, rg, rs, s1, r1, sb, p1, z2, p2, k1, k4, k4c, v1k, e6, coin, cvin, cot, cvt, cv,
+           asem, csem, sgsem, rgsem, s1sem, r1sem, ssem, rssem, p1s, p1r, p2s, p2r):
     me = lax.axis_index('dev')
     frag = lax.axis_index('frag')
+    core = lax.rem(me, 2)
+    mx = lax.rem(me // 2, 2)
+    my = me // 4
+    sib = me + 1 - 2 * core
+    xn = me + 2 - 4 * mx
+    yn = me + 4 - 8 * my
+    dg = xn + 4 - 8 * my
+    cols = [me, xn, yn, dg]
 
     def a_copies(p):
         slot = lax.rem(p, NBUF)
@@ -56,6 +69,9 @@
         slot = lax.rem(p, NBUF)
         pltpu.make_async_copy(a_ref.at[p], abuf.at[slot], asem.at[slot]).wait()
 
+    cin = [pltpu.make_async_copy(co_ref, coin, csem.at[0]), pltpu.make_async_copy(cv_ref, cvin, csem.at[1])]
+    for c in cin:
+        c.start()
     for p in range(NBUF - 1):
         a_start(p)
 
@@ -65,8 +81,10 @@
 
     cot[...] = jnp.zeros(cot.shape, BF)
     cvt[...] = jnp.zeros(cvt.shape, BF)
-    cot[0:NO, 0:NQ] = co_ref[...]
-    cvt[0:NV, 0:NQ] = cv_ref[...]
+    for c in cin:
+        c.wait()
+    cot[0:NO, 0:NQ] = coin[...]
+    cvt[0:NV, 0:NQ] = cvin[...]
     cv[...] = mm_nt(one_hot(iota((128, 128), 0) == iota((128, 128), 1)), cvt[...]).astype(BF)
     xr = mm(one_hot((iota((64, 16), 0) >> 3) == iota((64, 16), 1)), cot[...]).astype(BF)
     diff = iota((128, 960), 1) - iota((128, 960), 0)
@@ -80,17 +98,19 @@
         col = iota((128, 128), 1)
         w = mm(pi, one_hot(iota((128, 128), 0) == (col >> 4) + 8 * c))
         k4[:, c * 128:(c + 1) * 128] = jnp.where((iota((128, 128), 0) >> 3) == (col & 15), w, 0.0).astype(BF)
+    for h, d in enumerate((me, sib)):
+        col = iota((128, 240), 1)
+        w = mm(pi, one_hot(iota((128, 240), 0) == (col >> 4) + NP * d))
+        keep = (iota((128, 240), 0) >> 3) == (col & 15)
+        k4c[h] = jnp.where(keep, w, 0.0).astype(BF)
     e6[...] = one_hot((iota((128, 960), 1) >> 3) == iota((128, 960), 0))
 
-    def v1_rows(t, carry):
+    def v1_rows(t):
         row = iota((96, 128), 0) + 96 * t
         z = mm(one_hot((row >> 3) == iota((96, 128), 1)), cvt[...]).astype(BF)
         w = mm(z, e6[...])
         keep = (iota((96, 960), 0) & 7) == (iota((96, 960), 1) & 7)
         v1k[pl.ds(pl.multiple_of(96 * t, 96), 96), :] = jnp.where(keep, w, 0.0).astype(BF)
-        return carry
-
-    lax.fori_loop(0, 9, v1_rows, 0)
 
     pl.semaphore_wait(barrier, ND - 1)
 
@@ -126,17 +146,21 @@
         for k in range(1, ND):
             dst = lax.rem(me + k, ND)
             out.append(pltpu.make_async_remote_copy(
-                src_ref=sg.at[dst, p], dst_ref=rg.at[me, p], send_sem=sgsem.at[k], recv_sem=rgsem.at[me],
+                src_ref=sg.at[dst, p, 0:EX], dst_ref=rg.at[me, p], send_sem=sgsem.at[k], recv_sem=rgsem.at[me],
                 device_id=(frag, dst), device_id_type=MESH))
             out.append(pltpu.make_async_remote_copy(
                 src_ref=s1.at[dst, p], dst_ref=r1.at[me, p], send_sem=s1sem.at[k], recv_sem=r1sem.at[me],
                 device_id=(frag, dst), device_id_type=MESH))
+        for k in range(4):
+            out.append(pltpu.make_async_remote_copy(
+                src_ref=sg.at[cols[k] + 1 - 2 * core, p, EX:112], dst_ref=rs.at[k, p],
+                send_sem=ssem, recv_sem=rssem, device_id=(frag, sib), device_id_type=MESH))
         return out
 
     def send(p):
         for c in sends(p):
             c.start()
-        rg[me, p] = sg[me, p]
+        rg[me, p] = sg[me, p, 0:EX]
         r1[me, p] = s1[me, p]
 
     a_wait(0)
@@ -155,6 +179,11 @@
         a_wait(p)
         step1(p)
         step23(p - 1)
+
+        @pl.when(p < 10)
+        def _():
+            v1_rows(p - 1)
+
         return carry
 
     lax.fori_loop(1, NP, body, 0)
@@ -162,10 +191,41 @@
     step23(NP - 1)
     send(NP - 1)
 
+    def rcopy(src, dst, ss, rr, dev):
+        return pltpu.make_async_remote_copy(src_ref=src, dst_ref=dst, send_sem=ss, recv_sem=rr,
+                                            device_id=(frag, dev), device_id_type=MESH)
+
+    def bwait(view, sem):
+        pltpu.make_async_copy(view, view, sem).wait()
+
+    bwait(rs, rssem)
+    for u, v in ((1, 3), (2, 0)):
+        for b in range(AB - NE):
+            side = []
+            for c in (u, v):
+                own = sg[cols[c], :, EX + 16 * b:EX + 16 * b + 16, :].reshape(240, 128)
+                oth = rs[c, :, 16 * b:16 * b + 16, :].reshape(240, 128)
+                side.append((own, oth))
+            w = (mm(k4c[0], jnp.concatenate([side[0][0], side[1][0]], axis=1))
+                 + mm(k4c[1], jnp.concatenate([side[0][1], side[1][1]], axis=1)))
+            n = min(128, RSR - 128 * b)
+            sb[u, 128 * b:128 * b + n, :] = w[:n, :128]
+            sb[v, 128 * b:128 * b + n, :] = w[:n, 128:]
+
+    def rows(half, c):
+        return pl.ds((half * NCH + c) * CH, CH)
+
+    first = ((1, xn, yn, 2), (2, yn, xn, 1))
+    for c in range(NCH):
+        for half, (col, peer, _, _) in enumerate(first):
+            for m, cc in enumerate((col, 3)):
+                rcopy(sb.at[cc, rows(half, c)], p1.at[m, rows(half, c)],
+                      p1s.at[half, c], p1r.at[half, c], peer).start()
+
     for k in range(1, ND):
         src = lax.rem(me + k, ND)
-        pltpu.make_async_copy(r1.at[src], r1.at[src], r1sem.at[src]).wait()
-        pltpu.make_async_copy(rg.at[src], rg.at[src], rgsem.at[src]).wait()
+        bwait(r1.at[src], r1sem.at[src])
+        bwait(rg.at[src], rgsem.at[src])
 
     v = r1[...].reshape(960, 128)
 
@@ -176,21 +236,35 @@
 
     lax.fori_loop(0, 9, v1_out, 0)
 
-    for ab in range(0, AB, 2):
+    for ab in range(0, NE, 2):
         left = rg[:, :, 16 * ab:16 * ab + 16, :].reshape(1920, 128)
-        if ab + 1 < AB:
-            right = rg[:, :, 16 * ab + 16:16 * ab + 32, :].reshape(1920, 128)
-            w = mm(k4[...], jnp.concatenate([left, right], axis=1)).reshape(16, 8, 256)
-            o2_ref[16 * ab:16 * ab + 16] = w[:, :, :NV]
-            o2_ref[16 * ab + 16:16 * ab + 32] = w[:, :, 128:128 + NV]
-        else:
-            w = mm(k4[...], left).reshape(16, 8, 128)
-            o2_ref[16 * ab:NV] = w[:NV - 16 * ab, :, :NV]
+        right = rg[:, :, 16 * ab + 16:16 * ab + 32, :].reshape(1920, 128)
+        w = mm(k4[...], jnp.concatenate([left, right], axis=1)).reshape(16, 8, 256)
+        o2_ref[16 * ab:16 * ab + 16] = w[:, :, :NV]
+        o2_ref[16 * ab + 16:16 * ab + 32] = w[:, :, 128:128 + NV]
+
+    for c in range(NCH):
+        for half, (_, _, peer, col) in enumerate(first):
+            bwait(p1.at[:, rows(half, c)], p1r.at[half, c])
+            z2[rows(half, c), :] = sb[col, rows(half, c), :] + p1[1, rows(half, c), :]
+        for half, (_, _, peer, col) in enumerate(first):
+            rcopy(z2.at[rows(half, c)], p2.at[rows(half, c)], p2s.at[half, c], p2r.at[half, c], peer).start()
+    for c in range(NCH):
+        for half in range(2):
+            bwait(p2.at[rows(half, c)], p2r.at[half, c])
+            w = sb[0, rows(half, c), :] + p1[0, rows(half, c), :] + p2[rows(half, c), :]
+            a0 = EX + (half * NCH + c) * CH // 8
+            o2_ref[a0:a0 + CH // 8] = w.reshape(CH // 8, 8, 128)[:, :, :NV]
 
     for k in range(1, ND):
         dst = lax.rem(me + k, ND)
-        pltpu.make_async_copy(sg.at[dst], sg.at[dst], sgsem.at[k]).wait()
-        pltpu.make_async_copy(s1.at[dst], s1.at[dst], s1sem.at[k]).wait()
+        bwait(rg.at[dst], sgsem.at[k])
+        bwait(s1.at[dst], s1sem.at[k])
+    bwait(rs, ssem)
+    for c in range(NCH):
+        for half in range(2):
+            bwait(p1.at[:, rows(half, c)], p1s.at[half, c])
+            bwait(p2.at[rows(half, c)], p2s.at[half, c])
 
 
 def solution(mesh):
@@ -200,30 +274,45 @@
         o1, o2 = pl.pallas_call(
             kernel,
             out_shape=[jax.ShapeDtypeStruct((NV, NO, NV), F32), jax.ShapeDtypeStruct((NV, NO, NV), F32)],
-            in_specs=[pl.BlockSpec(memory_space=pl.ANY), vm, vm],
+            in_specs=[pl.BlockSpec(memory_space=pltpu.HBM)] * 3,
             out_specs=[vm, vm],
             scratch_shapes=[
                 pltpu.VMEM((NBUF, ROWS, NQ), BF),
                 pltpu.VMEM((2, 8, 128, 128), BF),
                 pltpu.VMEM((8, NP, 112, 128), BF),
-                pltpu.VMEM((8, NP, 112, 128), BF),
+                pltpu.VMEM((8, NP, EX, 128), BF),
+                pltpu.VMEM((4, NP, 112 - EX, 128), BF),
                 pltpu.VMEM((8, NP, 8, 128), BF),
                 pltpu.VMEM((8, NP, 8, 128), BF),
+                pltpu.VMEM((4, RSR, 128), F32),
+                pltpu.VMEM((2, RSR, 128), F32),
+                pltpu.VMEM((RSR, 128), F32),
+                pltpu.VMEM((RSR, 128), F32),
                 pltpu.VMEM((64, 960), BF),
                 pltpu.VMEM((128, 1920), BF),
+                pltpu.VMEM((2, 128, 240), BF),
                 pltpu.VMEM((864, 960), BF),
                 pltpu.VMEM((128, 960), BF),
+                pltpu.VMEM((NO, NQ), BF),
+                pltpu.VMEM((NV, NQ), BF),
                 pltpu.VMEM((16, 128), BF),
                 pltpu.VMEM((128, 128), BF),
                 pltpu.VMEM((128, 128), BF),
                 pltpu.SemaphoreType.DMA((NBUF,)),
+                pltpu.SemaphoreType.DMA((2,)),
                 pltpu.SemaphoreType.DMA((ND,)),
                 pltpu.SemaphoreType.DMA((ND,)),
                 pltpu.SemaphoreType.DMA((ND,)),
                 pltpu.SemaphoreType.DMA((ND,)),
+                pltpu.SemaphoreType.DMA,
+                pltpu.SemaphoreType.DMA,
+                pltpu.SemaphoreType.DMA((2, NCH)),
+                pltpu.SemaphoreType.DMA((2, NCH)),
+                pltpu.SemaphoreType.DMA((2, NCH)),
+                pltpu.SemaphoreType.DMA((2, NCH)),
             ],
             compiler_params=pltpu.CompilerParams(collective_id=0, has_side_effects=True,
-                                                 vmem_limit_bytes=60 * 1024 * 1024),
+                                                 vmem_limit_bytes=34 * 1024 * 1024),
             name='mo_blocks',
         )(a, co.T, cv.T)
         return o1.transpose(0, 2, 1), o2.transpose(1, 0, 2)

time: 57.9 us -> 46.8 us (0.81)
  Pallas kernels: 53.5 us -> 43 us
  local copies, waits for them, and re-layouts: 3.61 us -> 2.95 us
    pallas_call x1, Pallas kernels: 53.5 us -> 43 us  [local_part(): pl.pallas_call(kernel, out_shape=[jax.ShapeDtypeStruct((NV, NO, NV), F32)...]
    unnamed x2 -> x6, local copies, waits for them, and re-layouts: 3.61 us -> 2.95 us
where the time goes in v2:
time: 46.8 us; the launch traced here: 46.6 us
  Pallas kernels  43 us (92%)
  local copies, waits for them, and re-layouts  2.95 us (6%)
  between operations  0.65 us (1%)
    pallas_call x1, Pallas kernels, local_part(): pl.pallas_call(kernel, out_shape=[jax.ShapeDtypeStruct((NV, NO, NV), F32)...  43 us
    unnamed x6, local copies, waits for them, and re-layouts  2.95 us

profile of v2, /device:TPU:0, one launch (start us, length us, event | category | flops | bytes accessed | tf_op | source)
XLA Modules:
  0.0 46.6 jit_solution(13586207728397571970)
XLA Ops:
  0.6 0.0 copy-start
  0.6 0.7 %copy-done = bf16[120,108]{0,1:T(8,128)(2,1)S(1)} copy-done((bf16[120,108]{0,1:T(8,128)(2,1)S(1)}, bf16[120,108]{0,1:T(8,128)(2,1)}, u32[]{:S(2)}) %copy-start) | copy-done | bytes 25944
  1.4 0.0 copy-start.1
  1.4 0.7 %copy-done.1 = bf16[120,8]{0,1:T(8,128)(2,1)S(1)} copy-done((bf16[120,8]{0,1:T(8,128)(2,1)S(1)}, bf16[120,8]{0,1:T(8,128)(2,1)}, u32[]{:S(2)}) %copy-start.1) | copy-done | bytes 1944
  2.1 43.0 %mo_blocks.1 = (f32[108,8,108]{2,1,0:T(8,128)S(1)}, f32[108,8,108]{2,1,0:T(8,128)S(1)}) custom-call(bf16[15,14400,120]{2,1,0:T(8,128)(2,1)} %bitcast.9, bf16[8,120]{1,0:T(8,128)(2,1)S(1)} %bitcast.8, bf16[108,120]{1,0:T(8,128)(2,1)S(1)} %bitcast.7), custom_call_target="tpu_custom_call" | custom-call | tf_op jit(solution)/shard_map/mo_blocks/pallas_call | solution.py:274
  45.1 0.8 %copy.7 = f32[108,108,8]{1,2,0:T(8,128)} copy(f32[108,108,8]{1,2,0:T(8,128)S(1)} %bitcast.6) | data formatting | bytes 746496
  45.8 0.8 %copy.8 = f32[8,108,108]{2,0,1:T(8,128)} copy(f32[8,108,108]{2,0,1:T(8,128)S(1)} %bitcast.5) | data formatting | bytes 746496
Async XLA Ops:
  0.6 0.7 %copy-start = (bf16[120,108]{0,1:T(8,128)(2,1)S(1)}, bf16[120,108]{0,1:T(8,128)(2,1)}, u32[]{:S(2)}) copy-start(bf16[120,108]{0,1:T(8,128)(2,1)} %param.5) | copy-start | bytes 77764
  1.4 0.7 %copy-start.1 = (bf16[120,8]{0,1:T(8,128)(2,1)S(1)}, bf16[120,8]{0,1:T(8,128)(2,1)}, u32[]{:S(2)}) copy-start(bf16[120,8]{0,1:T(8,128)(2,1)} %param.4) | copy-start | bytes 5764

commit v3 on v2

--- a/solution.py
+++ b/solution.py
@@ -19,6 +19,10 @@
 AB = 7
 NE = 2
 EX = 16 * NE
+GO = EX
+SENT = EX + 8
+RS0 = EX + 16
+XR = 128
 RSR = 8 * (NV - EX)
 NCH = 2
 CH = RSR // (2 * NCH)
@@ -41,8 +45,8 @@
 
 
 def kernel(a_ref, co_ref, cv_ref, o1_ref, o2_ref,
-           abuf, tbuf, sg, rg, rs, s1, r1, sb, p1, z2, p2, k1, k4, k4c, v1k, e6, coin, cvin, cot, cvt, cv,
-           asem, csem, sgsem, rgsem, s1sem, r1sem, ssem, rssem, p1s, p1r, p2s, p2r):
+           abuf, tbuf, sg, rg, rs, sb, p1, z2, p2, k1, k4, k4c, v1k, e6, coin, cvin, cot, cvt, cv,
+           asem, csem, sgsem, rgsem, ssem, rssem, p1s, p1r, p2s, p2r):
     me = lax.axis_index('dev')
     frag = lax.axis_index('frag')
     core = lax.rem(me, 2)
@@ -94,24 +98,11 @@
     off = iota((64, 960), 1) - 120 * (iota((64, 960), 0) & 7)
     k1[...] = jnp.where((off >= 0) & (off < 120), mm(xr, one_hot(hit)), 0.0).astype(BF)
     pi = mm(one_hot((iota((128, 16), 0) & 7) == iota((128, 16), 1)), cot[...]).astype(BF)
-    for c in range(15):
-        col = iota((128, 128), 1)
-        w = mm(pi, one_hot(iota((128, 128), 0) == (col >> 4) + 8 * c))
-        k4[:, c * 128:(c + 1) * 128] = jnp.where((iota((128, 128), 0) >> 3) == (col & 15), w, 0.0).astype(BF)
     for h, d in enumerate((me, sib)):
         col = iota((128, 240), 1)
         w = mm(pi, one_hot(iota((128, 240), 0) == (col >> 4) + NP * d))
         keep = (iota((128, 240), 0) >> 3) == (col & 15)
         k4c[h] = jnp.where(keep, w, 0.0).astype(BF)
-    e6[...] = one_hot((iota((128, 960), 1) >> 3) == iota((128, 960), 0))
-
-    def v1_rows(t):
-        row = iota((96, 128), 0) + 96 * t
-        z = mm(one_hot((row >> 3) == iota((96, 128), 1)), cvt[...]).astype(BF)
-        w = mm(z, e6[...])
-        keep = (iota((96, 960), 0) & 7) == (iota((96, 960), 1) & 7)
-        v1k[pl.ds(pl.multiple_of(96 * t, 96), 96), :] = jnp.where(keep, w, 0.0).astype(BF)
-
     pl.semaphore_wait(barrier, ND - 1)
 
     def step1(p):
@@ -133,35 +124,33 @@
     def step23(p):
         t = tbuf[lax.rem(p, 2)].reshape(1024, 128)
         h = mm(t, cv[...]).astype(BF).reshape(8, 128, 128)
+        hoo = mm_nt(cot[...], t)
         for x in range(0, 8, 2):
             g = mm(cvt[0:112, :], jnp.concatenate([h[x], h[x + 1]], axis=1)).astype(BF)
-            sg[x, p] = g[:, :128]
-            sg[x + 1, p] = g[:, 128:]
-        hoo = mm_nt(cot[...], t)
+            for y in range(2):
+                sg[x // 2, y, p, 0:EX] = g[0:EX, 128 * y:128 * y + 128]
+                sg[x // 2, y, p, RS0:RS0 + 112 - EX] = g[EX:, 128 * y:128 * y + 128]
         hoo = jnp.concatenate([hoo[0:8, 128 * x:128 * x + 128] for x in range(8)], axis=0).astype(BF)
-        s1[:, p] = mm(hoo, cv[...]).astype(BF).reshape(8, 8, 128)
+        goo = mm(hoo, cv[...]).astype(BF).reshape(4, 2, 8, 128)
+        for y in range(2):
+            sg[:, y, p, GO:GO + 8] = goo[:, y]
 
     def sends(p):
-        out = []
+        out = [pltpu.make_async_remote_copy(
+            src_ref=sg.at[:, 1 - core, p, RS0:RS0 + 112 - EX], dst_ref=rs.at[:, p],
+            send_sem=ssem, recv_sem=rssem, device_id=(frag, sib), device_id_type=MESH)]
         for k in range(1, ND):
             dst = lax.rem(me + k, ND)
             out.append(pltpu.make_async_remote_copy(
-                src_ref=sg.at[dst, p, 0:EX], dst_ref=rg.at[me, p], send_sem=sgsem.at[k], recv_sem=rgsem.at[me],
-                device_id=(frag, dst), device_id_type=MESH))
-            out.append(pltpu.make_async_remote_copy(
-                src_ref=s1.at[dst, p], dst_ref=r1.at[me, p], send_sem=s1sem.at[k], recv_sem=r1sem.at[me],
-                device_id=(frag, dst), device_id_type=MESH))
-        for k in range(4):
-            out.append(pltpu.make_async_remote_copy(
-                src_ref=sg.at[cols[k] + 1 - 2 * core, p, EX:112], dst_ref=rs.at[k, p],
-                send_sem=ssem, recv_sem=rssem, device_id=(frag, sib), device_id_type=MESH))
+                src_ref=sg.at[dst // 2, lax.rem(dst, 2), p, 0:SENT], dst_ref=rg.at[me, p, 0:SENT],
+                send_sem=sgsem.at[k], recv_sem=rgsem.at[me], device_id=(frag, dst), device_id_type=MESH))
         return out
 
     def send(p):
         for c in sends(p):
             c.start()
-        rg[me, p] = sg[me, p, 0:EX]
-        r1[me, p] = s1[me, p]
+        rg[me, p, 0:EX] = sg[me // 2, core, p, 0:EX]
+        rg[me, p, GO:GO + 8] = sg[me // 2, core, p, GO:GO + 8]
 
     a_wait(0)
     a_start(NBUF - 1)
@@ -177,13 +166,8 @@
             send(p - 2)
 
         a_wait(p)
+        step23(p - 1)
         step1(p)
-        step23(p - 1)
-
-        @pl.when(p < 10)
-        def _():
-            v1_rows(p - 1)
-
         return carry
 
     lax.fori_loop(1, NP, body, 0)
@@ -203,8 +187,8 @@
         for b in range(AB - NE):
             side = []
             for c in (u, v):
-                own = sg[cols[c], :, EX + 16 * b:EX + 16 * b + 16, :].reshape(240, 128)
-                oth = rs[c, :, 16 * b:16 * b + 16, :].reshape(240, 128)
+                own = sg[cols[c] // 2, core, :, RS0 + 16 * b:RS0 + 16 * b + 16, :].reshape(240, 128)
+                oth = rs[cols[c] // 2, :, 16 * b:16 * b + 16, :].reshape(240, 128)
                 side.append((own, oth))
             w = (mm(k4c[0], jnp.concatenate([side[0][0], side[1][0]], axis=1))
                  + mm(k4c[1], jnp.concatenate([side[0][1], side[1][1]], axis=1)))
@@ -222,12 +206,29 @@
                 rcopy(sb.at[cc, rows(half, c)], p1.at[m, rows(half, c)],
                       p1s.at[half, c], p1r.at[half, c], peer).start()
 
+    for c in range(15):
+        col = iota((128, 128), 1)
+        w = mm(pi, one_hot(iota((128, 128), 0) == (col >> 4) + 8 * c))
+        k4[:, c * 128:(c + 1) * 128] = jnp.where((iota((128, 128), 0) >> 3) == (col & 15), w, 0.0).astype(BF)
+    e6[...] = one_hot((iota((128, 960), 1) >> 3) == iota((128, 960), 0))
+
+    def v1_rows(t):
+        row = iota((96, 128), 0) + 96 * t
+        z = mm(one_hot((row >> 3) == iota((96, 128), 1)), cvt[...]).astype(BF)
+        w = mm(z, e6[...])
+        keep = (iota((96, 960), 0) & 7) == (iota((96, 960), 1) & 7)
+        v1k[pl.ds(pl.multiple_of(96 * t, 96), 96), :] = jnp.where(keep, w, 0.0).astype(BF)
+
+    def v1_build(t, carry):
+        v1_rows(t)
+        return carry
+
+    lax.fori_loop(0, 9, v1_build, 0)
     for k in range(1, ND):
         src = lax.rem(me + k, ND)
-        bwait(r1.at[src], r1sem.at[src])
-        bwait(rg.at[src], rgsem.at[src])
-
-    v = r1[...].reshape(960, 128)
+        bwait(rg.at[src, :, 0:SENT], rgsem.at[src])
+
+    v = rg[:, :, GO:GO + 8, :].reshape(960, 128)
 
     def v1_out(t, carry):
         w = mm(v1k[pl.ds(pl.multiple_of(96 * t, 96), 96), :], v)
@@ -258,8 +259,7 @@
 
     for k in range(1, ND):
         dst = lax.rem(me + k, ND)
-        bwait(rg.at[dst], sgsem.at[k])
-        bwait(s1.at[dst], s1sem.at[k])
+        bwait(rg.at[dst, :, 0:SENT], sgsem.at[k])
     bwait(rs, ssem)
     for c in range(NCH):
         for half in range(2):
@@ -267,9 +267,18 @@
             bwait(p2.at[rows(half, c)], p2s.at[half, c])
 
 
+def write_out(x1_ref, x2_ref, y1_ref, y2_ref, sem):
+    copies = [pltpu.make_async_copy(x1_ref, y1_ref, sem.at[0]), pltpu.make_async_copy(x2_ref, y2_ref, sem.at[1])]
+    for c in copies:
+        c.start()
+    for c in copies:
+        c.wait()
+
+
 def solution(mesh):
     def local_part(ao, co, cv):
         a = ao.reshape(NP, ROWS, NQ)
+        co, cv = (pltpu.with_memory_space_constraint(t.T, pltpu.HBM) for t in (co, cv))
         vm = pl.BlockSpec(memory_space=pltpu.VMEM)
         o1, o2 = pl.pallas_call(
             kernel,
@@ -279,11 +288,9 @@
             scratch_shapes=[
                 pltpu.VMEM((NBUF, ROWS, NQ), BF),
                 pltpu.VMEM((2, 8, 128, 128), BF),
-                pltpu.VMEM((8, NP, 112, 128), BF),
-                pltpu.VMEM((8, NP, EX, 128), BF),
+                pltpu.VMEM((4, 2, NP, XR, 128), BF),
+                pltpu.VMEM((8, NP, EX + 16, 128), BF),
                 pltpu.VMEM((4, NP, 112 - EX, 128), BF),
-                pltpu.VMEM((8, NP, 8, 128), BF),
-                pltpu.VMEM((8, NP, 8, 128), BF),
                 pltpu.VMEM((4, RSR, 128), F32),
                 pltpu.VMEM((2, RSR, 128), F32),
                 pltpu.VMEM((RSR, 128), F32),
@@ -302,8 +309,6 @@
                 pltpu.SemaphoreType.DMA((2,)),
                 pltpu.SemaphoreType.DMA((ND,)),
                 pltpu.SemaphoreType.DMA((ND,)),
-                pltpu.SemaphoreType.DMA((ND,)),
-                pltpu.SemaphoreType.DMA((ND,)),
                 pltpu.SemaphoreType.DMA,
                 pltpu.SemaphoreType.DMA,
                 pltpu.SemaphoreType.DMA((2, NCH)),
@@ -314,7 +319,16 @@
             compiler_params=pltpu.CompilerParams(collective_id=0, has_side_effects=True,
                                                  vmem_limit_bytes=34 * 1024 * 1024),
             name='mo_blocks',
-        )(a, co.T, cv.T)
+        )(a, co, cv)
+        o1, o2 = pl.pallas_call(
+            write_out,
+            out_shape=[jax.ShapeDtypeStruct((NV, NO, NV), F32), jax.ShapeDtypeStruct((NV, NO, NV), F32)],
+            in_specs=[vm, vm],
+            out_specs=[pl.BlockSpec(memory_space=pltpu.HBM)] * 2,
+            scratch_shapes=[pltpu.SemaphoreType.DMA((2,))],
+            compiler_params=pltpu.CompilerParams(vmem_limit_bytes=2 * 1024 * 1024),
+            name='write_out',
+        )(o1, o2)
         return o1.transpose(0, 2, 1), o2.transpose(1, 0, 2)
 
     return jax.shard_map(local_part, mesh=mesh,

time: 46.8 us -> 40.3 us (0.86)
  Pallas kernels: 43 us -> 39.5 us
  local copies, waits for them, and re-layouts: 2.95 us -> 0 us
    pallas_call x1, Pallas kernels: 43 us -> 38.6 us  [local_part(): pl.pallas_call(kernel, out_shape=[jax.ShapeDtypeStruct((NV, NO, NV), F32)...]
    unnamed x6 -> x0, local copies, waits for them, and re-layouts: 2.95 us -> none
    pallas_call x0 -> x1, Pallas kernels: none -> 0.93 us  [local_part(): pl.pallas_call(write_out, out_shape=[jax.ShapeDtypeStruct((NV, NO, NV), F...]
where the time goes in v3:
time: 40.3 us; the launch traced here: 40.2 us
  Pallas kernels  39.5 us (98%)
  between operations  0.64 us (2%)
    pallas_call x1, Pallas kernels, local_part(): pl.pallas_call(kernel, out_shape=[jax.ShapeDtypeStruct((NV, NO, NV), F32)...  38.6 us
    pallas_call x1, Pallas kernels, local_part(): pl.pallas_call(write_out, out_shape=[jax.ShapeDtypeStruct((NV, NO, NV), F...  0.93 us

profile of v3, /device:TPU:0, one launch (start us, length us, event | category | flops | bytes accessed | tf_op | source)
XLA Modules:
  0.0 40.2 jit_solution(12950504912967248170)
XLA Ops:
  0.6 38.6 %mo_blocks.1 = (f32[108,8,108]{2,1,0:T(8,128)S(1)}, f32[108,8,108]{2,1,0:T(8,128)S(1)}) custom-call(bf16[15,14400,120]{2,1,0:T(8,128)(2,1)} %bitcast.5, bf16[8,120]{1,0:T(8,128)(2,1)} %bitcast.7, bf16[108,120]{1,0:T(8,128)(2,1)} %bitcast.6), custom_call_target="tpu_custom_call" | custom-call | tf_op jit(solution)/shard_map/mo_blocks/pallas_call | solution.py:283
  39.3 0.9 %write_out.1 = (f32[108,8,108]{2,1,0:T(8,128)}, f32[108,8,108]{2,1,0:T(8,128)}) custom-call(f32[108,8,108]{2,1,0:T(8,128)S(1)} %get-tuple-element.6.x1_ref, f32[108,8,108]{2,1,0:T(8,128)S(1)} %get-tuple-element.7.x2_ref), custom_call_target="tpu_custom_call" | custom-call | tf_op jit(solution)/shard_map/write_out/pallas_call | solution.py:323

commit v4 on v3

--- a/solution.py
+++ b/solution.py
@@ -17,7 +17,7 @@
 NBUF = 4
 SPLIT = 5
 AB = 7
-NE = 2
+NE = 1
 EX = 16 * NE
 GO = EX
 SENT = EX + 8
@@ -25,7 +25,8 @@
 XR = 128
 RSR = 8 * (NV - EX)
 NCH = 2
-CH = RSR // (2 * NCH)
+HALF = RSR // 16 * 8
+CUTS = [[0, HALF // 16 * 8, HALF], [HALF, HALF + (RSR - HALF) // 16 * 8, RSR]]
 
 
 def mm(a, b):
@@ -197,7 +198,7 @@
             sb[v, 128 * b:128 * b + n, :] = w[:n, 128:]
 
     def rows(half, c):
-        return pl.ds((half * NCH + c) * CH, CH)
+        return slice(CUTS[half][c], CUTS[half][c + 1])
 
     first = ((1, xn, yn, 2), (2, yn, xn, 1))
     for c in range(NCH):
@@ -238,11 +239,11 @@
     lax.fori_loop(0, 9, v1_out, 0)
 
     for ab in range(0, NE, 2):
-        left = rg[:, :, 16 * ab:16 * ab + 16, :].reshape(1920, 128)
-        right = rg[:, :, 16 * ab + 16:16 * ab + 32, :].reshape(1920, 128)
-        w = mm(k4[...], jnp.concatenate([left, right], axis=1)).reshape(16, 8, 256)
-        o2_ref[16 * ab:16 * ab + 16] = w[:, :, :NV]
-        o2_ref[16 * ab + 16:16 * ab + 32] = w[:, :, 128:128 + NV]
+        n = min(2, NE - ab)
+        w = mm(k4[...], jnp.concatenate([rg[:, :, 16 * (ab + u):16 * (ab + u) + 16, :].reshape(1920, 128)
+                                         for u in range(n)], axis=1)).reshape(16, 8, 128 * n)
+        for u in range(n):
+            o2_ref[16 * (ab + u):16 * (ab + u) + 16] = w[:, :, 128 * u:128 * u + NV]
 
     for c in range(NCH):
         for half, (_, _, peer, col) in enumerate(first):
@@ -254,8 +255,8 @@
         for half in range(2):
             bwait(p2.at[rows(half, c)], p2r.at[half, c])
             w = sb[0, rows(half, c), :] + p1[0, rows(half, c), :] + p2[rows(half, c), :]
-            a0 = EX + (half * NCH + c) * CH // 8
-            o2_ref[a0:a0 + CH // 8] = w.reshape(CH // 8, 8, 128)[:, :, :NV]
+            a0, a1 = EX + CUTS[half][c] // 8, EX + CUTS[half][c + 1] // 8
+            o2_ref[a0:a1] = w.reshape(a1 - a0, 8, 128)[:, :, :NV]
 
     for k in range(1, ND):
         dst = lax.rem(me + k, ND)

time: 40.3 us -> 42.1 us (1.045)
  Pallas kernels: 39.5 us -> 41.4 us
    pallas_call x1, Pallas kernels: 38.6 us -> 40.4 us  [local_part(): pl.pallas_call(kernel, out_shape=[jax.ShapeDtypeStruct((NV, NO, NV), F32)...]
where the time goes in v4:
time: 42.1 us; the launch traced here: 42 us
  Pallas kernels  41.4 us (98%)
  between operations  0.64 us (2%)
    pallas_call x1, Pallas kernels, local_part(): pl.pallas_call(kernel, out_shape=[jax.ShapeDtypeStruct((NV, NO, NV), F32)...  40.4 us
    pallas_call x1, Pallas kernels, local_part(): pl.pallas_call(write_out, out_shape=[jax.ShapeDtypeStruct((NV, NO, NV), F...  0.93 us

profile of v4, /device:TPU:0, one launch (start us, length us, event | category | flops | bytes accessed | tf_op | source)
XLA Modules:
  0.0 42.0 jit_solution(10524518587768978594)
XLA Ops:
  0.6 40.4 %mo_blocks.1 = (f32[108,8,108]{2,1,0:T(8,128)S(1)}, f32[108,8,108]{2,1,0:T(8,128)S(1)}) custom-call(bf16[15,14400,120]{2,1,0:T(8,128)(2,1)} %bitcast.5, bf16[8,120]{1,0:T(8,128)(2,1)} %bitcast.7, bf16[108,120]{1,0:T(8,128)(2,1)} %bitcast.6), custom_call_target="tpu_custom_call" | custom-call | tf_op jit(solution)/shard_map/mo_blocks/pallas_call | solution.py:284
  41.1 0.9 %write_out.1 = (f32[108,8,108]{2,1,0:T(8,128)}, f32[108,8,108]{2,1,0:T(8,128)}) custom-call(f32[108,8,108]{2,1,0:T(8,128)S(1)} %get-tuple-element.6.x1_ref, f32[108,8,108]{2,1,0:T(8,128)S(1)} %get-tuple-element.7.x2_ref), custom_call_target="tpu_custom_call" | custom-call | tf_op jit(solution)/shard_map/write_out/pallas_call | solution.py:324

commit v5 on v4

--- a/solution.py
+++ b/solution.py
@@ -17,7 +17,7 @@
 NBUF = 4
 SPLIT = 5
 AB = 7
-NE = 1
+NE = 3
 EX = 16 * NE
 GO = EX
 SENT = EX + 8

time: 42.1 us -> 40.2 us (0.955)
  Pallas kernels: 41.4 us -> 39.5 us
    pallas_call x1, Pallas kernels: 40.4 us -> 38.6 us  [local_part(): pl.pallas_call(kernel, out_shape=[jax.ShapeDtypeStruct((NV, NO, NV), F32)...]
where the time goes in v5:
time: 40.2 us; the launch traced here: 40.1 us
  Pallas kernels  39.5 us (98%)
  between operations  0.64 us (2%)
    pallas_call x1, Pallas kernels, local_part(): pl.pallas_call(kernel, out_shape=[jax.ShapeDtypeStruct((NV, NO, NV), F32)...  38.6 us
    pallas_call x1, Pallas kernels, local_part(): pl.pallas_call(write_out, out_shape=[jax.ShapeDtypeStruct((NV, NO, NV), F...  0.93 us

profile of v5, /device:TPU:0, one launch (start us, length us, event | category | flops | bytes accessed | tf_op | source)
XLA Modules:
  0.0 40.1 jit_solution(2041341174617501704)
XLA Ops:
  0.6 38.6 %mo_blocks.1 = (f32[108,8,108]{2,1,0:T(8,128)S(1)}, f32[108,8,108]{2,1,0:T(8,128)S(1)}) custom-call(bf16[15,14400,120]{2,1,0:T(8,128)(2,1)} %bitcast.5, bf16[8,120]{1,0:T(8,128)(2,1)} %bitcast.7, bf16[108,120]{1,0:T(8,128)(2,1)} %bitcast.6), custom_call_target="tpu_custom_call" | custom-call | tf_op jit(solution)/shard_map/mo_blocks/pallas_call | solution.py:284
  39.2 0.9 %write_out.1 = (f32[108,8,108]{2,1,0:T(8,128)}, f32[108,8,108]{2,1,0:T(8,128)}) custom-call(f32[108,8,108]{2,1,0:T(8,128)S(1)} %get-tuple-element.6.x1_ref, f32[108,8,108]{2,1,0:T(8,128)S(1)} %get-tuple-element.7.x2_ref), custom_call_target="tpu_custom_call" | custom-call | tf_op jit(solution)/shard_map/write_out/pallas_call | solution.py:324

commit v6 on v5

--- a/solution.py
+++ b/solution.py
@@ -16,14 +16,16 @@
 ROWS = NQ * NQ
 NBUF = 4
 SPLIT = 5
-AB = 7
-NE = 3
+VB = 6
+GR = 16 * VB
+GC = 20
+NE = 2
 EX = 16 * NE
 GO = EX
 SENT = EX + 8
 RS0 = EX + 16
-XR = 128
-RSR = 8 * (NV - EX)
+RS1 = RS0 + GR - EX
+RSR = 8 * (GR - EX)
 NCH = 2
 HALF = RSR // 16 * 8
 CUTS = [[0, HALF // 16 * 8, HALF], [HALF, HALF + (RSR - HALF) // 16 * 8, RSR]]
@@ -126,11 +128,15 @@
         t = tbuf[lax.rem(p, 2)].reshape(1024, 128)
         h = mm(t, cv[...]).astype(BF).reshape(8, 128, 128)
         hoo = mm_nt(cot[...], t)
+        lane = iota((16, 128), 1)
         for x in range(0, 8, 2):
-            g = mm(cvt[0:112, :], jnp.concatenate([h[x], h[x + 1]], axis=1)).astype(BF)
+            g = mm(cvt[0:112, :], jnp.concatenate([h[x], h[x + 1]], axis=1))
             for y in range(2):
-                sg[x // 2, y, p, 0:EX] = g[0:EX, 128 * y:128 * y + 128]
-                sg[x // 2, y, p, RS0:RS0 + 112 - EX] = g[EX:, 128 * y:128 * y + 128]
+                last = g[GR:GR + 16, 128 * y:128 * y + 128]
+                tiles = [jnp.where(lane < NV, g[16 * k:16 * k + 16, 128 * y:128 * y + 128],
+                                   pltpu.roll(last, (NV - GC * k) % 128, 1)) for k in range(VB)]
+                sg[x // 2, y, p, 0:EX] = jnp.concatenate(tiles[:NE], axis=0).astype(BF)
+                sg[x // 2, y, p, RS0:RS1] = jnp.concatenate(tiles[NE:], axis=0).astype(BF)
         hoo = jnp.concatenate([hoo[0:8, 128 * x:128 * x + 128] for x in range(8)], axis=0).astype(BF)
         goo = mm(hoo, cv[...]).astype(BF).reshape(4, 2, 8, 128)
         for y in range(2):
@@ -138,7 +144,7 @@
 
     def sends(p):
         out = [pltpu.make_async_remote_copy(
-            src_ref=sg.at[:, 1 - core, p, RS0:RS0 + 112 - EX], dst_ref=rs.at[:, p],
+            src_ref=sg.at[:, 1 - core, p, RS0:RS1], dst_ref=rs.at[:, p],
             send_sem=ssem, recv_sem=rssem, device_id=(frag, sib), device_id_type=MESH)]
         for k in range(1, ND):
             dst = lax.rem(me + k, ND)
@@ -185,7 +191,7 @@
 
     bwait(rs, rssem)
     for u, v in ((1, 3), (2, 0)):
-        for b in range(AB - NE):
+        for b in range(VB - NE):
             side = []
             for c in (u, v):
                 own = sg[cols[c] // 2, core, :, RS0 + 16 * b:RS0 + 16 * b + 16, :].reshape(240, 128)
@@ -193,9 +199,8 @@
                 side.append((own, oth))
             w = (mm(k4c[0], jnp.concatenate([side[0][0], side[1][0]], axis=1))
                  + mm(k4c[1], jnp.concatenate([side[0][1], side[1][1]], axis=1)))
-            n = min(128, RSR - 128 * b)
-            sb[u, 128 * b:128 * b + n, :] = w[:n, :128]
-            sb[v, 128 * b:128 * b + n, :] = w[:n, 128:]
+            sb[u, 128 * b:128 * b + 128, :] = w[:, :128]
+            sb[v, 128 * b:128 * b + 128, :] = w[:, 128:]
 
     def rows(half, c):
         return slice(CUTS[half][c], CUTS[half][c + 1])
@@ -207,6 +212,14 @@
                 rcopy(sb.at[cc, rows(half, c)], p1.at[m, rows(half, c)],
                       p1s.at[half, c], p1r.at[half, c], peer).start()
 
+    def put(w, a0):
+        o2_ref[a0:a0 + w.shape[0]] = w[:, :, :NV]
+        for k in range(VB):
+            lo, hi = max(a0, 16 * k), min(a0 + w.shape[0], 16 * k + NV - GR)
+            if lo < hi:
+                n = min(GC, NV - GC * k)
+                o2_ref[GR + lo - 16 * k:GR + hi - 16 * k, :, GC * k:GC * k + n] = w[lo - a0:hi - a0, :, NV:NV + n]
+
     for c in range(15):
         col = iota((128, 128), 1)
         w = mm(pi, one_hot(iota((128, 128), 0) == (col >> 4) + 8 * c))
@@ -243,7 +256,7 @@
         w = mm(k4[...], jnp.concatenate([rg[:, :, 16 * (ab + u):16 * (ab + u) + 16, :].reshape(1920, 128)
                                          for u in range(n)], axis=1)).reshape(16, 8, 128 * n)
         for u in range(n):
-            o2_ref[16 * (ab + u):16 * (ab + u) + 16] = w[:, :, 128 * u:128 * u + NV]
+            put(w[:, :, 128 * u:128 * u + 128], 16 * (ab + u))
 
     for c in range(NCH):
         for half, (_, _, peer, col) in enumerate(first):
@@ -255,8 +268,7 @@
         for half in range(2):
             bwait(p2.at[rows(half, c)], p2r.at[half, c])
             w = sb[0, rows(half, c), :] + p1[0, rows(half, c), :] + p2[rows(half, c), :]
-            a0, a1 = EX + CUTS[half][c] // 8, EX + CUTS[half][c + 1] // 8
-            o2_ref[a0:a1] = w.reshape(a1 - a0, 8, 128)[:, :, :NV]
+            put(w.reshape(-1, 8, 128), EX + CUTS[half][c] // 8)
 
     for k in range(1, ND):
         dst = lax.rem(me + k, ND)
@@ -289,9 +301,9 @@
             scratch_shapes=[
                 pltpu.VMEM((NBUF, ROWS, NQ), BF),
                 pltpu.VMEM((2, 8, 128, 128), BF),
-                pltpu.VMEM((4, 2, NP, XR, 128), BF),
+                pltpu.VMEM((4, 2, NP, RS1, 128), BF),
                 pltpu.VMEM((8, NP, EX + 16, 128), BF),
-                pltpu.VMEM((4, NP, 112 - EX, 128), BF),
+                pltpu.VMEM((4, NP, GR - EX, 128), BF),
                 pltpu.VMEM((4, RSR, 128), F32),
                 pltpu.VMEM((2, RSR, 128), F32),
                 pltpu.VMEM((RSR, 128), F32),

time: 40.2 us -> 39.1 us (0.973)
  Pallas kernels: 39.5 us -> 38.3 us
    pallas_call x1, Pallas kernels: 38.6 us -> 37.4 us  [local_part(): pl.pallas_call(kernel, out_shape=[jax.ShapeDtypeStruct((NV, NO, NV), F32)...]
where the time goes in v6:
time: 39.1 us; the launch traced here: 39 us
  Pallas kernels  38.3 us (98%)
  between operations  0.64 us (2%)
    pallas_call x1, Pallas kernels, local_part(): pl.pallas_call(kernel, out_shape=[jax.ShapeDtypeStruct((NV, NO, NV), F32)...  37.4 us
    pallas_call x1, Pallas kernels, local_part(): pl.pallas_call(write_out, out_shape=[jax.ShapeDtypeStruct((NV, NO, NV), F...  0.93 us

profile of v6, /device:TPU:0, one launch (start us, length us, event | category | flops | bytes accessed | tf_op | source)
XLA Modules:
  0.0 39.0 jit_solution(5055155617202126293)
XLA Ops:
  0.6 37.4 %mo_blocks.1 = (f32[108,8,108]{2,1,0:T(8,128)S(1)}, f32[108,8,108]{2,1,0:T(8,128)S(1)}) custom-call(bf16[15,14400,120]{2,1,0:T(8,128)(2,1)} %bitcast.5, bf16[8,120]{1,0:T(8,128)(2,1)} %bitcast.7, bf16[108,120]{1,0:T(8,128)(2,1)} %bitcast.6), custom_call_target="tpu_custom_call" | custom-call | tf_op jit(solution)/shard_map/mo_blocks/pallas_call | solution.py:296
  38.1 0.9 %write_out.1 = (f32[108,8,108]{2,1,0:T(8,128)}, f32[108,8,108]{2,1,0:T(8,128)}) custom-call(f32[108,8,108]{2,1,0:T(8,128)S(1)} %get-tuple-element.6.x1_ref, f32[108,8,108]{2,1,0:T(8,128)S(1)} %get-tuple-element.7.x2_ref), custom_call_target="tpu_custom_call" | custom-call | tf_op jit(solution)/shard_map/write_out/pallas_call | solution.py:336

commit v7 on v6

--- a/solution.py
+++ b/solution.py
@@ -27,8 +27,9 @@
 RS1 = RS0 + GR - EX
 RSR = 8 * (GR - EX)
 NCH = 2
-HALF = RSR // 16 * 8
-CUTS = [[0, HALF // 16 * 8, HALF], [HALF, HALF + (RSR - HALF) // 16 * 8, RSR]]
+HB = (VB - NE) // 2
+HALF = 128 * HB
+CH = HALF // NCH
 
 
 def mm(a, b):
@@ -189,28 +190,39 @@
     def bwait(view, sem):
         pltpu.make_async_copy(view, view, sem).wait()
 
+    units = [(3, 0), (3, 1), (1, 0), (2, 1), (2, 0), (1, 1), (0, 0), (0, 1)]
+
+    def part(buf, at, kc):
+        return mm(kc, jnp.concatenate([buf[at + (slice(None), slice(r, r + 16))].reshape(240, 128)
+                                       for r in range(0, 16 * HB, 16)], axis=1))
+
+    for c, half in units:
+        r = RS0 + 16 * HB * half
+        w = part(sg.at[:, :, :, r:r + 16 * HB], (cols[c] // 2, core), k4c[0])
+        for b in range(HB):
+            sb[c, HALF * half + 128 * b:HALF * half + 128 * b + 128, :] = w[:, 128 * b:128 * b + 128]
+
+    def half_rows(half):
+        return slice(HALF * half, HALF * half + HALF)
+
+    def rows(half, c):
+        return slice(HALF * half + CH * c, HALF * half + CH * c + CH)
+
+    def first(n):
+        c, half = units[n]
+        m = 1 if c == 3 else 0
+        return rcopy(sb.at[c, half_rows(half)], p1.at[m, half_rows(half)], p1s.at[half, m], p1r.at[half, m],
+                     (xn, yn)[half])
+
     bwait(rs, rssem)
-    for u, v in ((1, 3), (2, 0)):
-        for b in range(VB - NE):
-            side = []
-            for c in (u, v):
-                own = sg[cols[c] // 2, core, :, RS0 + 16 * b:RS0 + 16 * b + 16, :].reshape(240, 128)
-                oth = rs[cols[c] // 2, :, 16 * b:16 * b + 16, :].reshape(240, 128)
-                side.append((own, oth))
-            w = (mm(k4c[0], jnp.concatenate([side[0][0], side[1][0]], axis=1))
-                 + mm(k4c[1], jnp.concatenate([side[0][1], side[1][1]], axis=1)))
-            sb[u, 128 * b:128 * b + 128, :] = w[:, :128]
-            sb[v, 128 * b:128 * b + 128, :] = w[:, 128:]
-
-    def rows(half, c):
-        return slice(CUTS[half][c], CUTS[half][c + 1])
-
-    first = ((1, xn, yn, 2), (2, yn, xn, 1))
-    for c in range(NCH):
-        for half, (col, peer, _, _) in enumerate(first):
-            for m, cc in enumerate((col, 3)):
-                rcopy(sb.at[cc, rows(half, c)], p1.at[m, rows(half, c)],
-                      p1s.at[half, c], p1r.at[half, c], peer).start()
+    for n, (c, half) in enumerate(units):
+        r = 16 * HB * half
+        w = part(rs.at[:, :, r:r + 16 * HB], (cols[c] // 2,), k4c[1])
+        for b in range(HB):
+            at = slice(HALF * half + 128 * b, HALF * half + 128 * b + 128)
+            sb[c, at, :] = sb[c, at, :] + w[:, 128 * b:128 * b + 128]
+        if 1 <= n <= 4:
+            first(n - 1).start()
 
     def put(w, a0):
         o2_ref[a0:a0 + w.shape[0]] = w[:, :, :NV]
@@ -258,17 +270,21 @@
         for u in range(n):
             put(w[:, :, 128 * u:128 * u + 128], 16 * (ab + u))
 
+    for half in range(2):
+        bwait(p1.at[1, half_rows(half)], p1r.at[half, 1])
+        z2[half_rows(half), :] = sb[2 - half, half_rows(half), :] + p1[1, half_rows(half), :]
     for c in range(NCH):
-        for half, (_, _, peer, col) in enumerate(first):
-            bwait(p1.at[:, rows(half, c)], p1r.at[half, c])
-            z2[rows(half, c), :] = sb[col, rows(half, c), :] + p1[1, rows(half, c), :]
-        for half, (_, _, peer, col) in enumerate(first):
-            rcopy(z2.at[rows(half, c)], p2.at[rows(half, c)], p2s.at[half, c], p2r.at[half, c], peer).start()
+        for half in range(2):
+            rcopy(z2.at[rows(half, c)], p2.at[rows(half, c)], p2s.at[half, c], p2r.at[half, c],
+                  (yn, xn)[half]).start()
+    for half in range(2):
+        bwait(p1.at[0, half_rows(half)], p1r.at[half, 0])
+        sb[0, half_rows(half), :] = sb[0, half_rows(half), :] + p1[0, half_rows(half), :]
     for c in range(NCH):
         for half in range(2):
             bwait(p2.at[rows(half, c)], p2r.at[half, c])
-            w = sb[0, rows(half, c), :] + p1[0, rows(half, c), :] + p2[rows(half, c), :]
-            put(w.reshape(-1, 8, 128), EX + CUTS[half][c] // 8)
+            w = sb[0, rows(half, c), :] + p2[rows(half, c), :]
+            put(w.reshape(-1, 8, 128), EX + (HALF * half + CH * c) // 8)
 
     for k in range(1, ND):
         dst = lax.rem(me + k, ND)
@@ -276,8 +292,10 @@
     bwait(rs, ssem)
     for c in range(NCH):
         for half in range(2):
-            bwait(p1.at[:, rows(half, c)], p1s.at[half, c])
             bwait(p2.at[rows(half, c)], p2s.at[half, c])
+    for m in range(2):
+        for half in range(2):
+            bwait(p1.at[m, half_rows(half)], p1s.at[half, m])
 
 
 def write_out(x1_ref, x2_ref, y1_ref, y2_ref, sem):
@@ -324,8 +342,8 @@
                 pltpu.SemaphoreType.DMA((ND,)),
                 pltpu.SemaphoreType.DMA,
                 pltpu.SemaphoreType.DMA,
-                pltpu.SemaphoreType.DMA((2, NCH)),
-                pltpu.SemaphoreType.DMA((2, NCH)),
+                pltpu.SemaphoreType.DMA((2, 2)),
+                pltpu.SemaphoreType.DMA((2, 2)),
                 pltpu.SemaphoreType.DMA((2, NCH)),
                 pltpu.SemaphoreType.DMA((2, NCH)),
             ],

time: 39.1 us -> 38.2 us (0.977)
  Pallas kernels: 38.3 us -> 37.4 us
    pallas_call x1, Pallas kernels: 37.4 us -> 36.5 us  [local_part(): pl.pallas_call(kernel, out_shape=[jax.ShapeDtypeStruct((NV, NO, NV), F32)...]
where the time goes in v7:
time: 38.2 us; the launch traced here: 38.1 us
  Pallas kernels  37.4 us (98%)
  between operations  0.64 us (2%)
    pallas_call x1, Pallas kernels, local_part(): pl.pallas_call(kernel, out_shape=[jax.ShapeDtypeStruct((NV, NO, NV), F32)...  36.5 us
    pallas_call x1, Pallas kernels, local_part(): pl.pallas_call(write_out, out_shape=[jax.ShapeDtypeStruct((NV, NO, NV), F...  0.93 us

profile of v7, /device:TPU:0, one launch (start us, length us, event | category | flops | bytes accessed | tf_op | source)
XLA Modules:
  0.0 38.1 jit_solution(5863136161737775264)
XLA Ops:
  0.6 36.5 %mo_blocks.1 = (f32[108,8,108]{2,1,0:T(8,128)S(1)}, f32[108,8,108]{2,1,0:T(8,128)S(1)}) custom-call(bf16[15,14400,120]{2,1,0:T(8,128)(2,1)} %bitcast.5, bf16[8,120]{1,0:T(8,128)(2,1)} %bitcast.7, bf16[108,120]{1,0:T(8,128)(2,1)} %bitcast.6), custom_call_target="tpu_custom_call" | custom-call | tf_op jit(solution)/shard_map/mo_blocks/pallas_call | solution.py:314
  37.1 0.9 %write_out.1 = (f32[108,8,108]{2,1,0:T(8,128)}, f32[108,8,108]{2,1,0:T(8,128)}) custom-call(f32[108,8,108]{2,1,0:T(8,128)S(1)} %get-tuple-element.6.x1_ref, f32[108,8,108]{2,1,0:T(8,128)S(1)} %get-tuple-element.7.x2_ref), custom_call_target="tpu_custom_call" | custom-call | tf_op jit(solution)/shard_map/write_out/pallas_call | solution.py:354

commit v8 on v7

--- a/solution.py
+++ b/solution.py
@@ -19,16 +19,20 @@
 VB = 6
 GR = 16 * VB
 GC = 20
-NE = 2
-EX = 16 * NE
+EX = 40
+VB = 6
+GR = 16 * VB
+GC = 20
 GO = EX
 SENT = EX + 8
-RS0 = EX + 16
-RS1 = RS0 + GR - EX
-RSR = 8 * (GR - EX)
+RS0 = -(-SENT // 16) * 16
+RSA = GR - EX
+RSB = -(-RSA // 16)
+RS1 = RS0 + 16 * RSB
+RSR = 8 * RSA
 NCH = 2
-HB = (VB - NE) // 2
-HALF = 128 * HB
+HB = RSB // 2
+HALF = RSR // 2
 CH = HALF // NCH
 
 
@@ -61,6 +65,9 @@
     yn = me + 4 - 8 * my
     dg = xn + 4 - 8 * my
     cols = [me, xn, yn, dg]
+    chips = [c // 2 for c in cols]
+    peers = [(3, 0), (3, 1), (1, 0), (1, 1), (2, 0), (2, 1), (0, 1)]
+    par = [core, 1 - core]
 
     def a_copies(p):
         slot = lax.rem(p, NBUF)
@@ -136,8 +143,9 @@
                 last = g[GR:GR + 16, 128 * y:128 * y + 128]
                 tiles = [jnp.where(lane < NV, g[16 * k:16 * k + 16, 128 * y:128 * y + 128],
                                    pltpu.roll(last, (NV - GC * k) % 128, 1)) for k in range(VB)]
-                sg[x // 2, y, p, 0:EX] = jnp.concatenate(tiles[:NE], axis=0).astype(BF)
-                sg[x // 2, y, p, RS0:RS1] = jnp.concatenate(tiles[NE:], axis=0).astype(BF)
+                tiles = jnp.concatenate(tiles, axis=0)
+                sg[x // 2, y, p, 0:EX] = tiles[:EX].astype(BF)
+                sg[x // 2, y, p, RS0:RS0 + RSA] = tiles[EX:].astype(BF)
         hoo = jnp.concatenate([hoo[0:8, 128 * x:128 * x + 128] for x in range(8)], axis=0).astype(BF)
         goo = mm(hoo, cv[...]).astype(BF).reshape(4, 2, 8, 128)
         for y in range(2):
@@ -147,19 +155,20 @@
         out = [pltpu.make_async_remote_copy(
             src_ref=sg.at[:, 1 - core, p, RS0:RS1], dst_ref=rs.at[:, p],
             send_sem=ssem, recv_sem=rssem, device_id=(frag, sib), device_id_type=MESH)]
-        for k in range(1, ND):
-            dst = lax.rem(me + k, ND)
+        for k, (c, q) in enumerate(peers):
             out.append(pltpu.make_async_remote_copy(
-                src_ref=sg.at[dst // 2, lax.rem(dst, 2), p, 0:SENT], dst_ref=rg.at[me, p, 0:SENT],
-                send_sem=sgsem.at[k], recv_sem=rgsem.at[me], device_id=(frag, dst), device_id_type=MESH))
+                src_ref=sg.at[chips[c], par[q], p, 0:SENT], dst_ref=rg.at[me, p, 0:SENT],
+                send_sem=sgsem.at[k], recv_sem=rgsem.at[me],
+                device_id=(frag, 2 * chips[c] + par[q]), device_id_type=MESH))
         return out
 
     def send(p):
         for c in sends(p):
             c.start()
-        rg[me, p, 0:EX] = sg[me // 2, core, p, 0:EX]
-        rg[me, p, GO:GO + 8] = sg[me // 2, core, p, GO:GO + 8]
-
+        rg[me, p, 0:SENT] = sg[chips[0], core, p, 0:SENT]
+
+    if RS0 + RSA < RS1:
+        sg[:, :, :, RS0 + RSA:RS1, :] = jnp.zeros((4, 2, NP, RS1 - RS0 - RSA, 128), BF)
     a_wait(0)
     a_start(NBUF - 1)
     step1(0)
@@ -190,7 +199,7 @@
     def bwait(view, sem):
         pltpu.make_async_copy(view, view, sem).wait()
 
-    units = [(3, 0), (3, 1), (1, 0), (2, 1), (2, 0), (1, 1), (0, 0), (0, 1)]
+    units = [(3, 0), (3, 1), (1, 0), (2, 0), (2, 1), (1, 1), (0, 0), (0, 1)]
 
     def part(buf, at, kc):
         return mm(kc, jnp.concatenate([buf[at + (slice(None), slice(r, r + 16))].reshape(240, 128)
@@ -198,9 +207,9 @@
 
     for c, half in units:
         r = RS0 + 16 * HB * half
-        w = part(sg.at[:, :, :, r:r + 16 * HB], (cols[c] // 2, core), k4c[0])
+        w = part(sg.at[:, :, :, r:r + 16 * HB], (chips[c], core), k4c[0])
         for b in range(HB):
-            sb[c, HALF * half + 128 * b:HALF * half + 128 * b + 128, :] = w[:, 128 * b:128 * b + 128]
+            sb[c, 128 * (HB * half + b):128 * (HB * half + b) + 128, :] = w[:, 128 * b:128 * b + 128]
 
     def half_rows(half):
         return slice(HALF * half, HALF * half + HALF)
@@ -208,21 +217,21 @@
     def rows(half, c):
         return slice(HALF * half + CH * c, HALF * half + CH * c + CH)
 
-    def first(n):
-        c, half = units[n]
+    def first(c, half):
         m = 1 if c == 3 else 0
         return rcopy(sb.at[c, half_rows(half)], p1.at[m, half_rows(half)], p1s.at[half, m], p1r.at[half, m],
                      (xn, yn)[half])
 
+    sent_after = {1: (3, 0), 2: (3, 1), 3: (1, 0), 5: (2, 1)}
     bwait(rs, rssem)
     for n, (c, half) in enumerate(units):
         r = 16 * HB * half
-        w = part(rs.at[:, :, r:r + 16 * HB], (cols[c] // 2,), k4c[1])
+        w = part(rs.at[:, :, r:r + 16 * HB], (chips[c],), k4c[1])
         for b in range(HB):
-            at = slice(HALF * half + 128 * b, HALF * half + 128 * b + 128)
+            at = slice(128 * (HB * half + b), 128 * (HB * half + b) + 128)
             sb[c, at, :] = sb[c, at, :] + w[:, 128 * b:128 * b + 128]
-        if 1 <= n <= 4:
-            first(n - 1).start()
+        if n in sent_after:
+            first(*sent_after[n]).start()
 
     def put(w, a0):
         o2_ref[a0:a0 + w.shape[0]] = w[:, :, :NV]
@@ -263,12 +272,13 @@
 
     lax.fori_loop(0, 9, v1_out, 0)
 
-    for ab in range(0, NE, 2):
-        n = min(2, NE - ab)
+    nx = -(-EX // 16)
+    for ab in range(0, nx, 2):
+        n = min(2, nx - ab)
         w = mm(k4[...], jnp.concatenate([rg[:, :, 16 * (ab + u):16 * (ab + u) + 16, :].reshape(1920, 128)
                                          for u in range(n)], axis=1)).reshape(16, 8, 128 * n)
         for u in range(n):
-            put(w[:, :, 128 * u:128 * u + 128], 16 * (ab + u))
+            put(w[:min(16, EX - 16 * (ab + u)), :, 128 * u:128 * u + 128], 16 * (ab + u))
 
     for half in range(2):
         bwait(p1.at[1, half_rows(half)], p1r.at[half, 1])
@@ -286,9 +296,8 @@
             w = sb[0, rows(half, c), :] + p2[rows(half, c), :]
             put(w.reshape(-1, 8, 128), EX + (HALF * half + CH * c) // 8)
 
-    for k in range(1, ND):
-        dst = lax.rem(me + k, ND)
-        bwait(rg.at[dst, :, 0:SENT], sgsem.at[k])
+    for k in range(ND - 1):
+        bwait(rg.at[0, :, 0:SENT], sgsem.at[k])
     bwait(rs, ssem)
     for c in range(NCH):
         for half in range(2):
@@ -320,9 +329,9 @@
                 pltpu.VMEM((NBUF, ROWS, NQ), BF),
                 pltpu.VMEM((2, 8, 128, 128), BF),
                 pltpu.VMEM((4, 2, NP, RS1, 128), BF),
-                pltpu.VMEM((8, NP, EX + 16, 128), BF),
-                pltpu.VMEM((4, NP, GR - EX, 128), BF),
-                pltpu.VMEM((4, RSR, 128), F32),
+                pltpu.VMEM((8, NP, RS0, 128), BF),
+                pltpu.VMEM((4, NP, RS1 - RS0, 128), BF),
+                pltpu.VMEM((4, 128 * RSB, 128), F32),
                 pltpu.VMEM((2, RSR, 128), F32),
                 pltpu.VMEM((RSR, 128), F32),
                 pltpu.VMEM((RSR, 128), F32),

time: 38.2 us -> 37.5 us (0.982)
  Pallas kernels: 37.4 us -> 36.7 us
    pallas_call x1, Pallas kernels: 36.5 us -> 35.8 us  [local_part(): pl.pallas_call(kernel, out_shape=[jax.ShapeDtypeStruct((NV, NO, NV), F32)...]
where the time goes in v8:
time: 37.5 us; the launch traced here: 37.4 us
  Pallas kernels  36.7 us (98%)
  between operations  0.64 us (2%)
    pallas_call x1, Pallas kernels, local_part(): pl.pallas_call(kernel, out_shape=[jax.ShapeDtypeStruct((NV, NO, NV), F32)...  35.8 us
    pallas_call x1, Pallas kernels, local_part(): pl.pallas_call(write_out, out_shape=[jax.ShapeDtypeStruct((NV, NO, NV), F...  0.93 us

profile of v8, /device:TPU:0, one launch (start us, length us, event | category | flops | bytes accessed | tf_op | source)
XLA Modules:
  0.0 37.4 jit_solution(5195846568907779910)
XLA Ops:
  0.6 35.8 %mo_blocks.1 = (f32[108,8,108]{2,1,0:T(8,128)S(1)}, f32[108,8,108]{2,1,0:T(8,128)S(1)}) custom-call(bf16[15,14400,120]{2,1,0:T(8,128)(2,1)} %bitcast.5, bf16[8,120]{1,0:T(8,128)(2,1)} %bitcast.7, bf16[108,120]{1,0:T(8,128)(2,1)} %bitcast.6), custom_call_target="tpu_custom_call" | custom-call | tf_op jit(solution)/shard_map/mo_blocks/pallas_call | solution.py:323
  36.4 0.9 %write_out.1 = (f32[108,8,108]{2,1,0:T(8,128)}, f32[108,8,108]{2,1,0:T(8,128)}) custom-call(f32[108,8,108]{2,1,0:T(8,128)S(1)} %get-tuple-element.6.x1_ref, f32[108,8,108]{2,1,0:T(8,128)S(1)} %get-tuple-element.7.x2_ref), custom_call_target="tpu_custom_call" | custom-call | tf_op jit(solution)/shard_map/write_out/pallas_call | solution.py:363

commit v9 on v8

--- a/solution.py
+++ b/solution.py
@@ -151,21 +151,23 @@
         for y in range(2):
             sg[:, y, p, GO:GO + 8] = goo[:, y]
 
-    def sends(p):
+    def sends(p, n):
+        ps = pl.ds(p, n)
         out = [pltpu.make_async_remote_copy(
-            src_ref=sg.at[:, 1 - core, p, RS0:RS1], dst_ref=rs.at[:, p],
+            src_ref=sg.at[:, 1 - core, ps, RS0:RS1], dst_ref=rs.at[:, ps],
             send_sem=ssem, recv_sem=rssem, device_id=(frag, sib), device_id_type=MESH)]
         for k, (c, q) in enumerate(peers):
             out.append(pltpu.make_async_remote_copy(
-                src_ref=sg.at[chips[c], par[q], p, 0:SENT], dst_ref=rg.at[me, p, 0:SENT],
+                src_ref=sg.at[chips[c], par[q], ps, 0:SENT], dst_ref=rg.at[me, ps, 0:SENT],
                 send_sem=sgsem.at[k], recv_sem=rgsem.at[me],
                 device_id=(frag, 2 * chips[c] + par[q]), device_id_type=MESH))
         return out
 
-    def send(p):
-        for c in sends(p):
+    def send(p, n):
+        for c in sends(p, n):
             c.start()
-        rg[me, p, 0:SENT] = sg[chips[0], core, p, 0:SENT]
+        for q in range(n):
+            rg[me, p + q, 0:SENT] = sg[chips[0], core, p + q, 0:SENT]
 
     if RS0 + RSA < RS1:
         sg[:, :, :, RS0 + RSA:RS1, :] = jnp.zeros((4, 2, NP, RS1 - RS0 - RSA, 128), BF)
@@ -178,9 +180,13 @@
         def _():
             a_start(p + NBUF - 1)
 
-        @pl.when(p >= 2)
+        @pl.when(p == 2)
         def _():
-            send(p - 2)
+            send(0, 1)
+
+        @pl.when((p > 2) & (lax.rem(p, 2) == 0))
+        def _():
+            send(p - 3, 2)
 
         a_wait(p)
         step23(p - 1)
@@ -188,9 +194,9 @@
         return carry
 
     lax.fori_loop(1, NP, body, 0)
-    send(NP - 2)
+    send(NP - 2, 1)
     step23(NP - 1)
-    send(NP - 1)
+    send(NP - 1, 1)
 
     def rcopy(src, dst, ss, rr, dev):
         return pltpu.make_async_remote_copy(src_ref=src, dst_ref=dst, send_sem=ss, recv_sem=rr,

time: 37.5 us -> 37.9 us (1.011)
  Pallas kernels: 36.7 us -> 37.2 us
    pallas_call x1, Pallas kernels: 35.8 us -> 36.3 us  [local_part(): pl.pallas_call(kernel, out_shape=[jax.ShapeDtypeStruct((NV, NO, NV), F32)...]
where the time goes in v9:
time: 37.9 us; the launch traced here: 37.8 us
  Pallas kernels  37.2 us (98%)
  between operations  0.64 us (2%)
    pallas_call x1, Pallas kernels, local_part(): pl.pallas_call(kernel, out_shape=[jax.ShapeDtypeStruct((NV, NO, NV), F32)...  36.3 us
    pallas_call x1, Pallas kernels, local_part(): pl.pallas_call(write_out, out_shape=[jax.ShapeDtypeStruct((NV, NO, NV), F...  0.93 us

profile of v9, /device:TPU:0, one launch (start us, length us, event | category | flops | bytes accessed | tf_op | source)
XLA Modules:
  0.0 37.8 jit_solution(12707112282712480704)
XLA Ops:
  0.6 36.3 %mo_blocks.1 = (f32[108,8,108]{2,1,0:T(8,128)S(1)}, f32[108,8,108]{2,1,0:T(8,128)S(1)}) custom-call(bf16[15,14400,120]{2,1,0:T(8,128)(2,1)} %bitcast.5, bf16[8,120]{1,0:T(8,128)(2,1)} %bitcast.7, bf16[108,120]{1,0:T(8,128)(2,1)} %bitcast.6), custom_call_target="tpu_custom_call" | custom-call | tf_op jit(solution)/shard_map/mo_blocks/pallas_call | solution.py:329
  36.9 0.9 %write_out.1 = (f32[108,8,108]{2,1,0:T(8,128)}, f32[108,8,108]{2,1,0:T(8,128)}) custom-call(f32[108,8,108]{2,1,0:T(8,128)S(1)} %get-tuple-element.6.x1_ref, f32[108,8,108]{2,1,0:T(8,128)S(1)} %get-tuple-element.7.x2_ref), custom_call_target="tpu_custom_call" | custom-call | tf_op jit(solution)/shard_map/write_out/pallas_call | solution.py:369

commit v10 on v8

--- a/solution.py
+++ b/solution.py
@@ -66,7 +66,9 @@
     dg = xn + 4 - 8 * my
     cols = [me, xn, yn, dg]
     chips = [c // 2 for c in cols]
-    peers = [(3, 0), (3, 1), (1, 0), (1, 1), (2, 0), (2, 1), (0, 1)]
+    one = core * chips[1] + (1 - core) * chips[3]
+    two = core * chips[3] + (1 - core) * chips[1]
+    peers = [(one, 0), (chips[2], 0), (two, 0), (one, 1), (chips[2], 1), (two, 1), (chips[0], 1)]
     par = [core, 1 - core]
 
     def a_copies(p):
@@ -155,11 +157,11 @@
         out = [pltpu.make_async_remote_copy(
             src_ref=sg.at[:, 1 - core, p, RS0:RS1], dst_ref=rs.at[:, p],
             send_sem=ssem, recv_sem=rssem, device_id=(frag, sib), device_id_type=MESH)]
-        for k, (c, q) in enumerate(peers):
+        for k, (chip, q) in enumerate(peers):
             out.append(pltpu.make_async_remote_copy(
-                src_ref=sg.at[chips[c], par[q], p, 0:SENT], dst_ref=rg.at[me, p, 0:SENT],
+                src_ref=sg.at[chip, par[q], p, 0:SENT], dst_ref=rg.at[me, p, 0:SENT],
                 send_sem=sgsem.at[k], recv_sem=rgsem.at[me],
-                device_id=(frag, 2 * chips[c] + par[q]), device_id_type=MESH))
+                device_id=(frag, 2 * chip + par[q]), device_id_type=MESH))
         return out
 
     def send(p):

time: 37.5 us -> 37.5 us (level)
  no operation moved by 1% of the time
where the time goes in v10:
time: 37.5 us; the launch traced here: 37.4 us
  Pallas kernels  36.7 us (98%)
  between operations  0.64 us (2%)
    pallas_call x1, Pallas kernels, local_part(): pl.pallas_call(kernel, out_shape=[jax.ShapeDtypeStruct((NV, NO, NV), F32)...  35.8 us
    pallas_call x1, Pallas kernels, local_part(): pl.pallas_call(write_out, out_shape=[jax.ShapeDtypeStruct((NV, NO, NV), F...  0.93 us

profile of v10, /device:TPU:0, one launch (start us, length us, event | category | flops | bytes accessed | tf_op | source)
XLA Modules:
  0.0 37.4 jit_solution(16086184898001518444)
XLA Ops:
  0.6 35.8 %mo_blocks.1 = (f32[108,8,108]{2,1,0:T(8,128)S(1)}, f32[108,8,108]{2,1,0:T(8,128)S(1)}) custom-call(bf16[15,14400,120]{2,1,0:T(8,128)(2,1)} %bitcast.5, bf16[8,120]{1,0:T(8,128)(2,1)} %bitcast.7, bf16[108,120]{1,0:T(8,128)(2,1)} %bitcast.6), custom_call_target="tpu_custom_call" | custom-call | tf_op jit(solution)/shard_map/mo_blocks/pallas_call | solution.py:325
  36.4 0.9 %write_out.1 = (f32[108,8,108]{2,1,0:T(8,128)}, f32[108,8,108]{2,1,0:T(8,128)}) custom-call(f32[108,8,108]{2,1,0:T(8,128)S(1)} %get-tuple-element.6.x1_ref, f32[108,8,108]{2,1,0:T(8,128)S(1)} %get-tuple-element.7.x2_ref), custom_call_target="tpu_custom_call" | custom-call | tf_op jit(solution)/shard_map/write_out/pallas_call | solution.py:365

commit v11 on v10

--- a/solution.py
+++ b/solution.py
@@ -224,7 +224,7 @@
         return rcopy(sb.at[c, half_rows(half)], p1.at[m, half_rows(half)], p1s.at[half, m], p1r.at[half, m],
                      (xn, yn)[half])
 
-    sent_after = {1: (3, 0), 2: (3, 1), 3: (1, 0), 5: (2, 1)}
+    sent_after = {1: (3, 0), 2: (3, 1)}
     bwait(rs, rssem)
     for n, (c, half) in enumerate(units):
         r = 16 * HB * half
@@ -261,6 +261,9 @@
         return carry
 
     lax.fori_loop(0, 9, v1_build, 0)
+    for half, col in ((0, 1), (1, 2)):
+        bwait(p1.at[1, half_rows(half)], p1s.at[half, 1])
+        first(col, half).start()
     for k in range(1, ND):
         src = lax.rem(me + k, ND)
         bwait(rg.at[src, :, 0:SENT], rgsem.at[src])
@@ -304,9 +307,8 @@
     for c in range(NCH):
         for half in range(2):
             bwait(p2.at[rows(half, c)], p2s.at[half, c])
-    for m in range(2):
-        for half in range(2):
-            bwait(p1.at[m, half_rows(half)], p1s.at[half, m])
+    for half in range(2):
+        bwait(p1.at[0, half_rows(half)], p1s.at[half, 0])
 
 
 def write_out(x1_ref, x2_ref, y1_ref, y2_ref, sem):

time: 37.5 us -> 37.3 us (level)
  no operation moved by 1% of the time
where the time goes in v11:
time: 37.3 us
  Pallas kernels  36.6 us (98%)
  between operations  0.64 us (2%)
    pallas_call x1, Pallas kernels, local_part(): pl.pallas_call(kernel, out_shape=[jax.ShapeDtypeStruct((NV, NO, NV), F32)...  35.7 us
    pallas_call x1, Pallas kernels, local_part(): pl.pallas_call(write_out, out_shape=[jax.ShapeDtypeStruct((NV, NO, NV), F...  0.93 us

profile of v11, /device:TPU:0, one launch (start us, length us, event | category | flops | bytes accessed | tf_op | source)
XLA Modules:
  0.0 37.3 jit_solution(3100919605754779677)
XLA Ops:
  0.6 35.7 %mo_blocks.1 = (f32[108,8,108]{2,1,0:T(8,128)S(1)}, f32[108,8,108]{2,1,0:T(8,128)S(1)}) custom-call(bf16[15,14400,120]{2,1,0:T(8,128)(2,1)} %bitcast.5, bf16[8,120]{1,0:T(8,128)(2,1)} %bitcast.7, bf16[108,120]{1,0:T(8,128)(2,1)} %bitcast.6), custom_call_target="tpu_custom_call" | custom-call | tf_op jit(solution)/shard_map/mo_blocks/pallas_call | solution.py:327
  36.3 0.9 %write_out.1 = (f32[108,8,108]{2,1,0:T(8,128)}, f32[108,8,108]{2,1,0:T(8,128)}) custom-call(f32[108,8,108]{2,1,0:T(8,128)S(1)} %get-tuple-element.6.x1_ref, f32[108,8,108]{2,1,0:T(8,128)S(1)} %get-tuple-element.7.x2_ref), custom_call_target="tpu_custom_call" | custom-call | tf_op jit(solution)/shard_map/write_out/pallas_call | solution.py:367

commit v12 on v11

--- a/solution.py
+++ b/solution.py
@@ -53,7 +53,7 @@
 
 
 def kernel(a_ref, co_ref, cv_ref, o1_ref, o2_ref,
-           abuf, tbuf, sg, rg, rs, sb, p1, z2, p2, k1, k4, k4c, v1k, e6, coin, cvin, cot, cvt, cv,
+           abuf, ta, tb, sg, rg, rs, sb, p1, z2, p2, k1, k4, k4c, v1k, e6, coin, cvin, cot, cvt, cv,
            asem, csem, sgsem, rgsem, ssem, rssem, p1s, p1r, p2s, p2r):
     me = lax.axis_index('dev')
     frag = lax.axis_index('frag')
@@ -118,40 +118,68 @@
         k4c[h] = jnp.where(keep, w, 0.0).astype(BF)
     pl.semaphore_wait(barrier, ND - 1)
 
-    def step1(p):
+    pad = jnp.zeros((960, 8), BF)
+    lane = iota((16, 128), 1)
+
+    def step1(p, t, g):
         slot = lax.rem(p, NBUF)
-        tslot = lax.rem(p, 2)
-        pad = jnp.zeros((960, 8), BF)
-        for g in range(8):
-            left = jnp.concatenate([abuf[slot, 1920 * g:1920 * g + 960, :], pad], axis=1)
-            if g < 7:
-                right = jnp.concatenate([abuf[slot, 1920 * g + 960:1920 * g + 1920, :], pad], axis=1)
-                out = mm(k1[...], jnp.concatenate([left, right], axis=1))
-                lo = out[:, :128].reshape(8, 8, 128)
-                hi = out[:, 128:].reshape(8, 8, 128)
-            else:
-                lo = mm(k1[...], left).reshape(8, 8, 128)
-                hi = jnp.zeros((8, 8, 128), F32)
-            tbuf[tslot, :, 16 * g:16 * g + 16, :] = jnp.concatenate([lo, hi], axis=1).astype(BF)
-
-    def step23(p):
-        t = tbuf[lax.rem(p, 2)].reshape(1024, 128)
-        h = mm(t, cv[...]).astype(BF).reshape(8, 128, 128)
-        hoo = mm_nt(cot[...], t)
-        lane = iota((16, 128), 1)
-        for x in range(0, 8, 2):
-            g = mm(cvt[0:112, :], jnp.concatenate([h[x], h[x + 1]], axis=1))
-            for y in range(2):
-                last = g[GR:GR + 16, 128 * y:128 * y + 128]
-                tiles = [jnp.where(lane < NV, g[16 * k:16 * k + 16, 128 * y:128 * y + 128],
-                                   pltpu.roll(last, (NV - GC * k) % 128, 1)) for k in range(VB)]
-                tiles = jnp.concatenate(tiles, axis=0)
-                sg[x // 2, y, p, 0:EX] = tiles[:EX].astype(BF)
-                sg[x // 2, y, p, RS0:RS0 + RSA] = tiles[EX:].astype(BF)
-        hoo = jnp.concatenate([hoo[0:8, 128 * x:128 * x + 128] for x in range(8)], axis=0).astype(BF)
+        left = jnp.concatenate([abuf[slot, 1920 * g:1920 * g + 960, :], pad], axis=1)
+        if g < 7:
+            right = jnp.concatenate([abuf[slot, 1920 * g + 960:1920 * g + 1920, :], pad], axis=1)
+            out = mm(k1[...], jnp.concatenate([left, right], axis=1))
+            lo = out[:, :128].reshape(8, 8, 128)
+            hi = out[:, 128:].reshape(8, 8, 128)
+        else:
+            lo = mm(k1[...], left).reshape(8, 8, 128)
+            hi = jnp.zeros((8, 8, 128), F32)
+        t[:, 16 * g:16 * g + 16, :] = jnp.concatenate([lo, hi], axis=1).astype(BF)
+
+    def step2(t, x):
+        h = mm(t[x:x + 2].reshape(256, 128), cv[...]).astype(BF)
+        return jnp.concatenate([h[:128], h[128:]], axis=1)
+
+    def step3(p, x, h):
+        g = mm(cvt[0:112, :], h)
+        for y in range(2):
+            last = g[GR:GR + 16, 128 * y:128 * y + 128]
+            tiles = [jnp.where(lane < NV, g[16 * k:16 * k + 16, 128 * y:128 * y + 128],
+                               pltpu.roll(last, (NV - GC * k) % 128, 1)) for k in range(VB)]
+            tiles = jnp.concatenate(tiles, axis=0)
+            sg[x // 2, y, p, 0:EX] = tiles[:EX].astype(BF)
+            sg[x // 2, y, p, RS0:RS0 + RSA] = tiles[EX:].astype(BF)
+
+    def step2o(t):
+        hoo = mm_nt(cot[...], t[...].reshape(1024, 128))
+        return jnp.concatenate([hoo[0:8, 128 * x:128 * x + 128] for x in range(8)], axis=0).astype(BF)
+
+    def step3o(p, hoo):
         goo = mm(hoo, cv[...]).astype(BF).reshape(4, 2, 8, 128)
         for y in range(2):
             sg[:, y, p, GO:GO + 8] = goo[:, y]
+
+    def work(p, told, tnew):
+        def one(g):
+            if tnew is not None:
+                step1(p, tnew, g)
+
+        h0 = step2(told, 0)
+        one(0)
+        h1 = step2(told, 2)
+        one(1)
+        step3(p - 1, 0, h0)
+        h2 = step2(told, 4)
+        one(2)
+        step3(p - 1, 2, h1)
+        h3 = step2(told, 6)
+        one(3)
+        step3(p - 1, 4, h2)
+        hoo = step2o(told)
+        one(4)
+        step3(p - 1, 6, h3)
+        one(5)
+        step3o(p - 1, hoo)
+        one(6)
+        one(7)
 
     def sends(p):
         out = [pltpu.make_async_remote_copy(
@@ -173,25 +201,26 @@
         sg[:, :, :, RS0 + RSA:RS1, :] = jnp.zeros((4, 2, NP, RS1 - RS0 - RSA, 128), BF)
     a_wait(0)
     a_start(NBUF - 1)
-    step1(0)
-
-    def body(p, carry):
-        @pl.when(p + NBUF - 1 < NP)
-        def _():
-            a_start(p + NBUF - 1)
-
-        @pl.when(p >= 2)
-        def _():
-            send(p - 2)
-
-        a_wait(p)
-        step23(p - 1)
-        step1(p)
+    for g in range(8):
+        step1(0, ta, g)
+
+    def body(k, carry):
+        for p, told, tnew in ((2 * k + 1, ta, tb), (2 * k + 2, tb, ta)):
+            @pl.when(p + NBUF - 1 < NP)
+            def _():
+                a_start(p + NBUF - 1)
+
+            @pl.when(p >= 2)
+            def _():
+                send(p - 2)
+
+            a_wait(p)
+            work(p, told, tnew)
         return carry
 
-    lax.fori_loop(1, NP, body, 0)
+    lax.fori_loop(0, NP // 2, body, 0)
     send(NP - 2)
-    step23(NP - 1)
+    work(NP, ta, None)
     send(NP - 1)
 
     def rcopy(src, dst, ss, rr, dev):
@@ -331,7 +360,8 @@
             out_specs=[vm, vm],
             scratch_shapes=[
                 pltpu.VMEM((NBUF, ROWS, NQ), BF),
-                pltpu.VMEM((2, 8, 128, 128), BF),
+                pltpu.VMEM((8, 128, 128), BF),
+                pltpu.VMEM((8, 128, 128), BF),
                 pltpu.VMEM((4, 2, NP, RS1, 128), BF),
                 pltpu.VMEM((8, NP, RS0, 128), BF),
                 pltpu.VMEM((4, NP, RS1 - RS0, 128), BF),

time: 37.3 us -> 36.3 us (0.973)
  Pallas kernels: 36.6 us -> 35.5 us
    pallas_call x1, Pallas kernels: 35.7 us -> 34.6 us  [local_part(): pl.pallas_call(kernel, out_shape=[jax.ShapeDtypeStruct((NV, NO, NV), F32)...]
where the time goes in v12:
time: 36.3 us; the launch traced here: 36.2 us
  Pallas kernels  35.5 us (98%)
  between operations  0.64 us (2%)
    pallas_call x1, Pallas kernels, local_part(): pl.pallas_call(kernel, out_shape=[jax.ShapeDtypeStruct((NV, NO, NV), F32)...  34.6 us
    pallas_call x1, Pallas kernels, local_part(): pl.pallas_call(write_out, out_shape=[jax.ShapeDtypeStruct((NV, NO, NV), F...  0.93 us

profile of v12, /device:TPU:0, one launch (start us, length us, event | category | flops | bytes accessed | tf_op | source)
XLA Modules:
  0.0 36.2 jit_solution(477263280691626090)
XLA Ops:
  0.6 34.6 %mo_blocks.1 = (f32[108,8,108]{2,1,0:T(8,128)S(1)}, f32[108,8,108]{2,1,0:T(8,128)S(1)}) custom-call(bf16[15,14400,120]{2,1,0:T(8,128)(2,1)} %bitcast.5, bf16[8,120]{1,0:T(8,128)(2,1)} %bitcast.7, bf16[108,120]{1,0:T(8,128)(2,1)} %bitcast.6), custom_call_target="tpu_custom_call" | custom-call | tf_op jit(solution)/shard_map/mo_blocks/pallas_call | solution.py:356
  35.3 0.9 %write_out.1 = (f32[108,8,108]{2,1,0:T(8,128)}, f32[108,8,108]{2,1,0:T(8,128)}) custom-call(f32[108,8,108]{2,1,0:T(8,128)S(1)} %get-tuple-element.6.x1_ref, f32[108,8,108]{2,1,0:T(8,128)S(1)} %get-tuple-element.7.x2_ref), custom_call_target="tpu_custom_call" | custom-call | tf_op jit(solution)/shard_map/write_out/pallas_call | solution.py:397

commit v13 on v12

--- a/solution.py
+++ b/solution.py
@@ -15,7 +15,7 @@
 NV = 108
 ROWS = NQ * NQ
 NBUF = 4
-SPLIT = 5
+PIECES = [0, 3840, 7680, 11520, ROWS]
 VB = 6
 GR = 16 * VB
 GC = 20
@@ -71,20 +71,18 @@
     peers = [(one, 0), (chips[2], 0), (two, 0), (one, 1), (chips[2], 1), (two, 1), (chips[0], 1)]
     par = [core, 1 - core]
 
-    def a_copies(p):
+    def a_copy(p, k):
         slot = lax.rem(p, NBUF)
-        step = ROWS // SPLIT
-        return [pltpu.make_async_copy(a_ref.at[p, pl.ds(k * step, step)],
-                                      abuf.at[slot, pl.ds(k * step, step)],
-                                      asem.at[slot]) for k in range(SPLIT)]
+        r = slice(PIECES[k], PIECES[k + 1])
+        return pltpu.make_async_copy(a_ref.at[p, r], abuf.at[slot, r], asem.at[slot, k])
 
     def a_start(p):
-        for c in a_copies(p):
-            c.start()
-
-    def a_wait(p):
-        slot = lax.rem(p, NBUF)
-        pltpu.make_async_copy(a_ref.at[p], abuf.at[slot], asem.at[slot]).wait()
+        for k in range(4):
+            a_copy(p, k).start()
+
+    def a_wait(p, parts=range(4)):
+        for k in parts:
+            a_copy(p, k).wait()
 
     cin = [pltpu.make_async_copy(co_ref, coin, csem.at[0]), pltpu.make_async_copy(cv_ref, cvin, csem.at[1])]
     for c in cin:
@@ -157,7 +155,7 @@
         for y in range(2):
             sg[:, y, p, GO:GO + 8] = goo[:, y]
 
-    def work(p, told, tnew):
+    def work(p, told, tnew, late=False):
         def one(g):
             if tnew is not None:
                 step1(p, tnew, g)
@@ -174,6 +172,8 @@
         one(3)
         step3(p - 1, 4, h2)
         hoo = step2o(told)
+        if late:
+            a_wait(p, (2, 3))
         one(4)
         step3(p - 1, 6, h3)
         one(5)
@@ -181,21 +181,22 @@
         one(6)
         one(7)
 
-    def sends(p):
-        out = [pltpu.make_async_remote_copy(
+    def pair_copy(p):
+        return pltpu.make_async_remote_copy(
             src_ref=sg.at[:, 1 - core, p, RS0:RS1], dst_ref=rs.at[:, p],
-            send_sem=ssem, recv_sem=rssem, device_id=(frag, sib), device_id_type=MESH)]
+            send_sem=ssem, recv_sem=rssem, device_id=(frag, sib), device_id_type=MESH)
+
+    def exchange(p):
         for k, (chip, q) in enumerate(peers):
-            out.append(pltpu.make_async_remote_copy(
+            pltpu.make_async_remote_copy(
                 src_ref=sg.at[chip, par[q], p, 0:SENT], dst_ref=rg.at[me, p, 0:SENT],
                 send_sem=sgsem.at[k], recv_sem=rgsem.at[me],
-                device_id=(frag, 2 * chip + par[q]), device_id_type=MESH))
-        return out
+                device_id=(frag, 2 * chip + par[q]), device_id_type=MESH).start()
+        rg[me, p, 0:SENT] = sg[chips[0], core, p, 0:SENT]
 
     def send(p):
-        for c in sends(p):
-            c.start()
-        rg[me, p, 0:SENT] = sg[chips[0], core, p, 0:SENT]
+        pair_copy(p).start()
+        exchange(p)
 
     if RS0 + RSA < RS1:
         sg[:, :, :, RS0 + RSA:RS1, :] = jnp.zeros((4, 2, NP, RS1 - RS0 - RSA, 128), BF)
@@ -206,22 +207,34 @@
 
     def body(k, carry):
         for p, told, tnew in ((2 * k + 1, ta, tb), (2 * k + 2, tb, ta)):
-            @pl.when(p + NBUF - 1 < NP)
-            def _():
-                a_start(p + NBUF - 1)
-
-            @pl.when(p >= 2)
-            def _():
+            a_start(p + NBUF - 1)
+            if told is ta:
+                @pl.when(k > 0)
+                def _():
+                    send(p - 2)
+            else:
                 send(p - 2)
-
             a_wait(p)
             work(p, told, tnew)
         return carry
 
-    lax.fori_loop(0, NP // 2, body, 0)
-    send(NP - 2)
+    lax.fori_loop(0, (NP - NBUF) // 2, body, 0)
+    for p in range((NP - NBUF) // 2 * 2 + 1, NP):
+        told, tnew = (ta, tb) if p % 2 else (tb, ta)
+        if p + NBUF - 1 < NP:
+            a_start(p + NBUF - 1)
+        send(p - 2)
+        if p < NP - 1:
+            a_wait(p)
+            work(p, told, tnew)
+        else:
+            a_wait(p, (0, 1))
+            work(p, told, tnew, late=True)
+    pair_copy(NP - 2).start()
     work(NP, ta, None)
-    send(NP - 1)
+    pair_copy(NP - 1).start()
+    exchange(NP - 2)
+    exchange(NP - 1)
 
     def rcopy(src, dst, ss, rr, dev):
         return pltpu.make_async_remote_copy(src_ref=src, dst_ref=dst, send_sem=ss, recv_sem=rr,
@@ -379,7 +392,7 @@
                 pltpu.VMEM((16, 128), BF),
                 pltpu.VMEM((128, 128), BF),
                 pltpu.VMEM((128, 128), BF),
-                pltpu.SemaphoreType.DMA((NBUF,)),
+                pltpu.SemaphoreType.DMA((NBUF, 4)),
                 pltpu.SemaphoreType.DMA((2,)),
                 pltpu.SemaphoreType.DMA((ND,)),
                 pltpu.SemaphoreType.DMA((ND,)),

time: 36.3 us -> 36.4 us (level)
  no operation moved by 1% of the time
where the time goes in v13:
time: 36.4 us; the launch traced here: 36.3 us
  Pallas kernels  35.6 us (98%)
  between operations  0.64 us (2%)
    pallas_call x1, Pallas kernels, local_part(): pl.pallas_call(kernel, out_shape=[jax.ShapeDtypeStruct((NV, NO, NV), F32)...  34.7 us
    pallas_call x1, Pallas kernels, local_part(): pl.pallas_call(write_out, out_shape=[jax.ShapeDtypeStruct((NV, NO, NV), F...  0.93 us

profile of v13, /device:TPU:0, one launch (start us, length us, event | category | flops | bytes accessed | tf_op | source)
XLA Modules:
  0.0 36.3 jit_solution(10906581715226885021)
XLA Ops:
  0.6 34.7 %mo_blocks.1 = (f32[108,8,108]{2,1,0:T(8,128)S(1)}, f32[108,8,108]{2,1,0:T(8,128)S(1)}) custom-call(bf16[15,14400,120]{2,1,0:T(8,128)(2,1)} %bitcast.5, bf16[8,120]{1,0:T(8,128)(2,1)} %bitcast.7, bf16[108,120]{1,0:T(8,128)(2,1)} %bitcast.6), custom_call_target="tpu_custom_call" | custom-call | tf_op jit(solution)/shard_map/mo_blocks/pallas_call | solution.py:369
  35.3 0.9 %write_out.1 = (f32[108,8,108]{2,1,0:T(8,128)}, f32[108,8,108]{2,1,0:T(8,128)}) custom-call(f32[108,8,108]{2,1,0:T(8,128)S(1)} %get-tuple-element.6.x1_ref, f32[108,8,108]{2,1,0:T(8,128)S(1)} %get-tuple-element.7.x2_ref), custom_call_target="tpu_custom_call" | custom-call | tf_op jit(solution)/shard_map/write_out/pallas_call | solution.py:410

commit v14 on v12

--- a/solution.py
+++ b/solution.py
@@ -19,7 +19,7 @@
 VB = 6
 GR = 16 * VB
 GC = 20
-EX = 40
+EX = 32
 VB = 6
 GR = 16 * VB
 GC = 20

time: 36.3 us -> 36.7 us (1.011)
  Pallas kernels: 35.5 us -> 36 us
    pallas_call x1, Pallas kernels: 34.6 us -> 35 us  [local_part(): pl.pallas_call(kernel, out_shape=[jax.ShapeDtypeStruct((NV, NO, NV), F32)...]
where the time goes in v14:
time: 36.7 us; the launch traced here: 36.6 us
  Pallas kernels  36 us (98%)
  between operations  0.64 us (2%)
    pallas_call x1, Pallas kernels, local_part(): pl.pallas_call(kernel, out_shape=[jax.ShapeDtypeStruct((NV, NO, NV), F32)...  35 us
    pallas_call x1, Pallas kernels, local_part(): pl.pallas_call(write_out, out_shape=[jax.ShapeDtypeStruct((NV, NO, NV), F...  0.93 us

profile of v14, /device:TPU:0, one launch (start us, length us, event | category | flops | bytes accessed | tf_op | source)
XLA Modules:
  0.0 36.6 jit_solution(1752923545189142653)
XLA Ops:
  0.6 35.0 %mo_blocks.1 = (f32[108,8,108]{2,1,0:T(8,128)S(1)}, f32[108,8,108]{2,1,0:T(8,128)S(1)}) custom-call(bf16[15,14400,120]{2,1,0:T(8,128)(2,1)} %bitcast.5, bf16[8,120]{1,0:T(8,128)(2,1)} %bitcast.7, bf16[108,120]{1,0:T(8,128)(2,1)} %bitcast.6), custom_call_target="tpu_custom_call" | custom-call | tf_op jit(solution)/shard_map/mo_blocks/pallas_call | solution.py:356
  35.7 0.9 %write_out.1 = (f32[108,8,108]{2,1,0:T(8,128)}, f32[108,8,108]{2,1,0:T(8,128)}) custom-call(f32[108,8,108]{2,1,0:T(8,128)S(1)} %get-tuple-element.6.x1_ref, f32[108,8,108]{2,1,0:T(8,128)S(1)} %get-tuple-element.7.x2_ref), custom_call_target="tpu_custom_call" | custom-call | tf_op jit(solution)/shard_map/write_out/pallas_call | solution.py:397

commit v15 on v12

--- a/solution.py
+++ b/solution.py
@@ -15,7 +15,7 @@
 NV = 108
 ROWS = NQ * NQ
 NBUF = 4
-SPLIT = 5
+PIECE = 3840
 VB = 6
 GR = 16 * VB
 GC = 20
@@ -71,20 +71,16 @@
     peers = [(one, 0), (chips[2], 0), (two, 0), (one, 1), (chips[2], 1), (two, 1), (chips[0], 1)]
     par = [core, 1 - core]
 
-    def a_copies(p):
+    def a_start(p):
         slot = lax.rem(p, NBUF)
-        step = ROWS // SPLIT
-        return [pltpu.make_async_copy(a_ref.at[p, pl.ds(k * step, step)],
-                                      abuf.at[slot, pl.ds(k * step, step)],
-                                      asem.at[slot]) for k in range(SPLIT)]
-
-    def a_start(p):
-        for c in a_copies(p):
-            c.start()
-
-    def a_wait(p):
+        for k in range(4):
+            r = slice(PIECE * k, min(PIECE * k + PIECE, ROWS))
+            pltpu.make_async_copy(a_ref.at[p, r], abuf.at[slot, r], asem.at[slot, k // 2]).start()
+
+    def a_wait(p, half):
         slot = lax.rem(p, NBUF)
-        pltpu.make_async_copy(a_ref.at[p], abuf.at[slot], asem.at[slot]).wait()
+        r = slice(0, 2 * PIECE) if half == 0 else slice(2 * PIECE, ROWS)
+        pltpu.make_async_copy(a_ref.at[p, r], abuf.at[slot, r], asem.at[slot, half]).wait()
 
     cin = [pltpu.make_async_copy(co_ref, coin, csem.at[0]), pltpu.make_async_copy(cv_ref, cvin, csem.at[1])]
     for c in cin:
@@ -174,6 +170,8 @@
         one(3)
         step3(p - 1, 4, h2)
         hoo = step2o(told)
+        if tnew is not None:
+            a_wait(p, 1)
         one(4)
         step3(p - 1, 6, h3)
         one(5)
@@ -199,9 +197,11 @@
 
     if RS0 + RSA < RS1:
         sg[:, :, :, RS0 + RSA:RS1, :] = jnp.zeros((4, 2, NP, RS1 - RS0 - RSA, 128), BF)
-    a_wait(0)
+    a_wait(0, 0)
     a_start(NBUF - 1)
     for g in range(8):
+        if g == 4:
+            a_wait(0, 1)
         step1(0, ta, g)
 
     def body(k, carry):
@@ -214,7 +214,7 @@
             def _():
                 send(p - 2)
 
-            a_wait(p)
+            a_wait(p, 0)
             work(p, told, tnew)
         return carry
 
@@ -379,7 +379,7 @@
                 pltpu.VMEM((16, 128), BF),
                 pltpu.VMEM((128, 128), BF),
                 pltpu.VMEM((128, 128), BF),
-                pltpu.SemaphoreType.DMA((NBUF,)),
+                pltpu.SemaphoreType.DMA((NBUF, 2)),
                 pltpu.SemaphoreType.DMA((2,)),
                 pltpu.SemaphoreType.DMA((ND,)),
                 pltpu.SemaphoreType.DMA((ND,)),

time: 36.3 us -> 37.4 us (1.030)
  Pallas kernels: 35.5 us -> 36.7 us
    pallas_call x1, Pallas kernels: 34.6 us -> 35.7 us  [local_part(): pl.pallas_call(kernel, out_shape=[jax.ShapeDtypeStruct((NV, NO, NV), F32)...]
where the time goes in v15:
time: 37.4 us; the launch traced here: 37.3 us
  Pallas kernels  36.7 us (98%)
  between operations  0.64 us (2%)
    pallas_call x1, Pallas kernels, local_part(): pl.pallas_call(kernel, out_shape=[jax.ShapeDtypeStruct((NV, NO, NV), F32)...  35.7 us
    pallas_call x1, Pallas kernels, local_part(): pl.pallas_call(write_out, out_shape=[jax.ShapeDtypeStruct((NV, NO, NV), F...  0.93 us

profile of v15, /device:TPU:0, one launch (start us, length us, event | category | flops | bytes accessed | tf_op | source)
XLA Modules:
  0.0 37.3 jit_solution(6507685593952483360)
XLA Ops:
  0.6 35.7 %mo_blocks.1 = (f32[108,8,108]{2,1,0:T(8,128)S(1)}, f32[108,8,108]{2,1,0:T(8,128)S(1)}) custom-call(bf16[15,14400,120]{2,1,0:T(8,128)(2,1)} %bitcast.5, bf16[8,120]{1,0:T(8,128)(2,1)} %bitcast.7, bf16[108,120]{1,0:T(8,128)(2,1)} %bitcast.6), custom_call_target="tpu_custom_call" | custom-call | tf_op jit(solution)/shard_map/mo_blocks/pallas_call | solution.py:356
  36.4 0.9 %write_out.1 = (f32[108,8,108]{2,1,0:T(8,128)}, f32[108,8,108]{2,1,0:T(8,128)}) custom-call(f32[108,8,108]{2,1,0:T(8,128)S(1)} %get-tuple-element.6.x1_ref, f32[108,8,108]{2,1,0:T(8,128)S(1)} %get-tuple-element.7.x2_ref), custom_call_target="tpu_custom_call" | custom-call | tf_op jit(solution)/shard_map/write_out/pallas_call | solution.py:397

commit v16 on v12

--- a/solution.py
+++ b/solution.py
@@ -210,8 +210,11 @@
             def _():
                 a_start(p + NBUF - 1)
 
-            @pl.when(p >= 2)
-            def _():
+            if told is ta:
+                @pl.when(k > 0)
+                def _():
+                    send(p - 2)
+            else:
                 send(p - 2)
 
             a_wait(p)
@@ -293,6 +296,13 @@
     for half, col in ((0, 1), (1, 2)):
         bwait(p1.at[1, half_rows(half)], p1s.at[half, 1])
         first(col, half).start()
+    for half in range(2):
+        bwait(p1.at[1, half_rows(half)], p1r.at[half, 1])
+        z2[half_rows(half), :] = sb[2 - half, half_rows(half), :] + p1[1, half_rows(half), :]
+    for c in range(NCH):
+        for half in range(2):
+            rcopy(z2.at[rows(half, c)], p2.at[rows(half, c)], p2s.at[half, c], p2r.at[half, c],
+                  (yn, xn)[half]).start()
     for k in range(1, ND):
         src = lax.rem(me + k, ND)
         bwait(rg.at[src, :, 0:SENT], rgsem.at[src])
@@ -314,13 +324,6 @@
         for u in range(n):
             put(w[:min(16, EX - 16 * (ab + u)), :, 128 * u:128 * u + 128], 16 * (ab + u))
 
-    for half in range(2):
-        bwait(p1.at[1, half_rows(half)], p1r.at[half, 1])
-        z2[half_rows(half), :] = sb[2 - half, half_rows(half), :] + p1[1, half_rows(half), :]
-    for c in range(NCH):
-        for half in range(2):
-            rcopy(z2.at[rows(half, c)], p2.at[rows(half, c)], p2s.at[half, c], p2r.at[half, c],
-                  (yn, xn)[half]).start()
     for half in range(2):
         bwait(p1.at[0, half_rows(half)], p1r.at[half, 0])
         sb[0, half_rows(half), :] = sb[0, half_rows(half), :] + p1[0, half_rows(half), :]

time: 36.3 us -> 36.3 us (level)
  no operation moved by 1% of the time
where the time goes in v16:
time: 36.3 us; the launch traced here: 36.2 us
  Pallas kernels  35.6 us (98%)
  between operations  0.64 us (2%)
    pallas_call x1, Pallas kernels, local_part(): pl.pallas_call(kernel, out_shape=[jax.ShapeDtypeStruct((NV, NO, NV), F32)...  34.6 us
    pallas_call x1, Pallas kernels, local_part(): pl.pallas_call(write_out, out_shape=[jax.ShapeDtypeStruct((NV, NO, NV), F...  0.93 us

profile of v16, /device:TPU:0, one launch (start us, length us, event | category | flops | bytes accessed | tf_op | source)
XLA Modules:
  0.0 36.2 jit_solution(9301436939276496475)
XLA Ops:
  0.6 34.6 %mo_blocks.1 = (f32[108,8,108]{2,1,0:T(8,128)S(1)}, f32[108,8,108]{2,1,0:T(8,128)S(1)}) custom-call(bf16[15,14400,120]{2,1,0:T(8,128)(2,1)} %bitcast.5, bf16[8,120]{1,0:T(8,128)(2,1)} %bitcast.7, bf16[108,120]{1,0:T(8,128)(2,1)} %bitcast.6), custom_call_target="tpu_custom_call" | custom-call | tf_op jit(solution)/shard_map/mo_blocks/pallas_call | solution.py:359
  35.3 0.9 %write_out.1 = (f32[108,8,108]{2,1,0:T(8,128)}, f32[108,8,108]{2,1,0:T(8,128)}) custom-call(f32[108,8,108]{2,1,0:T(8,128)S(1)} %get-tuple-element.6.x1_ref, f32[108,8,108]{2,1,0:T(8,128)S(1)} %get-tuple-element.7.x2_ref), custom_call_target="tpu_custom_call" | custom-call | tf_op jit(solution)/shard_map/write_out/pallas_call | solution.py:400

commit v17 on v16

--- a/solution.py
+++ b/solution.py
@@ -32,8 +32,7 @@
 RSR = 8 * RSA
 NCH = 2
 HB = RSB // 2
-HALF = RSR // 2
-CH = HALF // NCH
+XROWS = 192
 
 
 def mm(a, b):
@@ -246,10 +245,12 @@
             sb[c, 128 * (HB * half + b):128 * (HB * half + b) + 128, :] = w[:, 128 * b:128 * b + 128]
 
     def half_rows(half):
-        return slice(HALF * half, HALF * half + HALF)
+        return slice(XROWS, RSR) if half else slice(0, XROWS)
 
     def rows(half, c):
-        return slice(HALF * half + CH * c, HALF * half + CH * c + CH)
+        h = half_rows(half)
+        n = (h.stop - h.start) // NCH
+        return slice(h.start + n * c, h.start + n * c + n)
 
     def first(c, half):
         m = 1 if c == 3 else 0
@@ -331,7 +332,7 @@
         for half in range(2):
             bwait(p2.at[rows(half, c)], p2r.at[half, c])
             w = sb[0, rows(half, c), :] + p2[rows(half, c), :]
-            put(w.reshape(-1, 8, 128), EX + (HALF * half + CH * c) // 8)
+            put(w.reshape(-1, 8, 128), EX + rows(half, c).start // 8)
 
     for k in range(ND - 1):
         bwait(rg.at[0, :, 0:SENT], sgsem.at[k])

time: 36.3 us -> 36.6 us (level)
  no operation moved by 1% of the time
where the time goes in v17:
time: 36.6 us; the launch traced here: 36.5 us
  Pallas kernels  35.9 us (98%)
  between operations  0.64 us (2%)
    pallas_call x1, Pallas kernels, local_part(): pl.pallas_call(kernel, out_shape=[jax.ShapeDtypeStruct((NV, NO, NV), F32)...  35 us
    pallas_call x1, Pallas kernels, local_part(): pl.pallas_call(write_out, out_shape=[jax.ShapeDtypeStruct((NV, NO, NV), F...  0.93 us

profile of v17, /device:TPU:0, one launch (start us, length us, event | category | flops | bytes accessed | tf_op | source)
XLA Modules:
  0.0 36.5 jit_solution(2784319651413528817)
XLA Ops:
  0.6 35.0 %mo_blocks.1 = (f32[108,8,108]{2,1,0:T(8,128)S(1)}, f32[108,8,108]{2,1,0:T(8,128)S(1)}) custom-call(bf16[15,14400,120]{2,1,0:T(8,128)(2,1)} %bitcast.5, bf16[8,120]{1,0:T(8,128)(2,1)} %bitcast.7, bf16[108,120]{1,0:T(8,128)(2,1)} %bitcast.6), custom_call_target="tpu_custom_call" | custom-call | tf_op jit(solution)/shard_map/mo_blocks/pallas_call | solution.py:360
  35.6 0.9 %write_out.1 = (f32[108,8,108]{2,1,0:T(8,128)}, f32[108,8,108]{2,1,0:T(8,128)}) custom-call(f32[108,8,108]{2,1,0:T(8,128)S(1)} %get-tuple-element.6.x1_ref, f32[108,8,108]{2,1,0:T(8,128)S(1)} %get-tuple-element.7.x2_ref), custom_call_target="tpu_custom_call" | custom-call | tf_op jit(solution)/shard_map/write_out/pallas_call | solution.py:401

commit v18 on v17

--- a/solution.py
+++ b/solution.py
@@ -32,7 +32,7 @@
 RSR = 8 * RSA
 NCH = 2
 HB = RSB // 2
-XROWS = 192
+XROWS = 240
 
 
 def mm(a, b):

time: 36.6 us -> 36.1 us (0.986)
  Pallas kernels: 35.9 us -> 35.4 us
    pallas_call x1, Pallas kernels: 35 us -> 34.5 us  [local_part(): pl.pallas_call(kernel, out_shape=[jax.ShapeDtypeStruct((NV, NO, NV), F32)...]
where the time goes in v18:
time: 36.1 us; the launch traced here: 36 us
  Pallas kernels  35.4 us (98%)
  between operations  0.64 us (2%)
    pallas_call x1, Pallas kernels, local_part(): pl.pallas_call(kernel, out_shape=[jax.ShapeDtypeStruct((NV, NO, NV), F32)...  34.5 us
    pallas_call x1, Pallas kernels, local_part(): pl.pallas_call(write_out, out_shape=[jax.ShapeDtypeStruct((NV, NO, NV), F...  0.93 us

profile of v18, /device:TPU:0, one launch (start us, length us, event | category | flops | bytes accessed | tf_op | source)
XLA Modules:
  0.0 36.0 jit_solution(9369596821714992685)
XLA Ops:
  0.6 34.5 %mo_blocks.1 = (f32[108,8,108]{2,1,0:T(8,128)S(1)}, f32[108,8,108]{2,1,0:T(8,128)S(1)}) custom-call(bf16[15,14400,120]{2,1,0:T(8,128)(2,1)} %bitcast.5, bf16[8,120]{1,0:T(8,128)(2,1)} %bitcast.7, bf16[108,120]{1,0:T(8,128)(2,1)} %bitcast.6), custom_call_target="tpu_custom_call" | custom-call | tf_op jit(solution)/shard_map/mo_blocks/pallas_call | solution.py:360
  35.1 0.9 %write_out.1 = (f32[108,8,108]{2,1,0:T(8,128)}, f32[108,8,108]{2,1,0:T(8,128)}) custom-call(f32[108,8,108]{2,1,0:T(8,128)S(1)} %get-tuple-element.6.x1_ref, f32[108,8,108]{2,1,0:T(8,128)S(1)} %get-tuple-element.7.x2_ref), custom_call_target="tpu_custom_call" | custom-call | tf_op jit(solution)/shard_map/write_out/pallas_call | solution.py:401

commit v19 on v18

--- a/solution.py
+++ b/solution.py
@@ -32,7 +32,7 @@
 RSR = 8 * RSA
 NCH = 2
 HB = RSB // 2
-XROWS = 240
+XROWS = 256
 
 
 def mm(a, b):

time: 36.1 us -> 36 us (level)
  no operation moved by 1% of the time
where the time goes in v19:
time: 36 us; the launch traced here: 35.9 us
  Pallas kernels  35.3 us (98%)
  between operations  0.64 us (2%)
    pallas_call x1, Pallas kernels, local_part(): pl.pallas_call(kernel, out_shape=[jax.ShapeDtypeStruct((NV, NO, NV), F32)...  34.4 us
    pallas_call x1, Pallas kernels, local_part(): pl.pallas_call(write_out, out_shape=[jax.ShapeDtypeStruct((NV, NO, NV), F...  0.93 us

profile of v19, /device:TPU:0, one launch (start us, length us, event | category | flops | bytes accessed | tf_op | source)
XLA Modules:
  0.0 35.9 jit_solution(13125244759470415105)
XLA Ops:
  0.6 34.4 %mo_blocks.1 = (f32[108,8,108]{2,1,0:T(8,128)S(1)}, f32[108,8,108]{2,1,0:T(8,128)S(1)}) custom-call(bf16[15,14400,120]{2,1,0:T(8,128)(2,1)} %bitcast.5, bf16[8,120]{1,0:T(8,128)(2,1)} %bitcast.7, bf16[108,120]{1,0:T(8,128)(2,1)} %bitcast.6), custom_call_target="tpu_custom_call" | custom-call | tf_op jit(solution)/shard_map/mo_blocks/pallas_call | solution.py:360
  35.0 0.9 %write_out.1 = (f32[108,8,108]{2,1,0:T(8,128)}, f32[108,8,108]{2,1,0:T(8,128)}) custom-call(f32[108,8,108]{2,1,0:T(8,128)S(1)} %get-tuple-element.6.x1_ref, f32[108,8,108]{2,1,0:T(8,128)S(1)} %get-tuple-element.7.x2_ref), custom_call_target="tpu_custom_call" | custom-call | tf_op jit(solution)/shard_map/write_out/pallas_call | solution.py:401
